TPU v7x, 8 devices: a whole 2x2x1 slice. The times are simulated.
8 devices in a mesh: data: 8 (over z, y, x, core).
Axes of the slice: x: 2, y: 2, z: 1, core: 2. Of those that a mesh axis runs over, the one named last changes fastest.
Arguments:
- h_a: bfloat16 [4096, 512], P('data')
- h_b: bfloat16 [4096, 512], P('data')
- w_one: bfloat16 [512, 2048], replicated
- w_two: bfloat16 [2048, 2048], replicated
- w_three: bfloat16 [2048, 2048], replicated
- gain_one: float32 [2048], replicated
- shift_one: float32 [2048], replicated
- gain_two: float32 [2048], replicated
- shift_two: float32 [2048], replicated
- lam_off: float32 [], replicated
Outputs:
- output 1: float32 [], replicated
- output 2: float32 [512, 2048], P('data')
- output 3: float32 [2048, 2048], P('data')
- output 4: float32 [2048, 2048], P('data')
- output 5: float32 [2048], replicated
- output 6: float32 [2048], replicated
- output 7: float32 [2048], replicated
- output 8: float32 [2048], replicated
All inputs are finite; a program needn't handle non-finite values.
Results may differ from a plain program's by a relative error of at most 0.00520155.
Values are sent between devices in bfloat16 or wider.
A program may use at most 1 GiB of HBM per device.

v0:
```python
import jax
import jax.numpy as jnp
from jax import lax
from jax.sharding import PartitionSpec as P

NORM_EPS = 1e-5
ROW_DIMS = (((0, 1), (0, 1)), ((), ()))
FIRST_DIMS = (((0,), (0,)), ((), ()))
LAST_DIMS = (((2,), (1,)), ((), ()))


def norm_forward(values, total_rows):
    col_sums = jnp.stack([jnp.sum(values, axis=1), jnp.sum(values * values, axis=1)])
    col_sums = lax.psum(col_sums, "data")
    col_mean = col_sums[0] / total_rows
    inv_std = lax.rsqrt(col_sums[1] / total_rows - col_mean * col_mean + NORM_EPS)
    return (values - col_mean[:, None, :]) * inv_std[:, None, :], inv_std


def norm_backward(grad_out, normed, inv_std, total_rows):
    col_sums = lax.psum(jnp.stack([jnp.sum(grad_out, axis=1), jnp.sum(grad_out * normed, axis=1)]), "data")
    grad_in = inv_std[:, None, :] * (grad_out - (col_sums[0][:, None, :] + normed * col_sums[1][:, None, :]) / total_rows)
    return grad_in, col_sums


def solution(mesh):
    shards = mesh.shape["data"]

    def local_step(h_a, h_b, w_one, w_two, w_three, gain_one, shift_one, gain_two, shift_two, lam_off):
        rows_dev = h_a.shape[0]
        total_rows = rows_dev * shards
        feat_rows = jnp.concatenate([h_a, h_b], axis=0)
        hidden_one = jnp.dot(feat_rows, w_one, preferred_element_type=jnp.float32).reshape(2, rows_dev, -1)
        normed_one, inv_one = norm_forward(hidden_one, total_rows)
        pre_one = gain_one * normed_one + shift_one
        act_one = jax.nn.relu(pre_one).astype(jnp.bfloat16)
        hidden_two = jnp.dot(act_one, w_two, preferred_element_type=jnp.float32)
        normed_two, inv_two = norm_forward(hidden_two, total_rows)
        pre_two = gain_two * normed_two + shift_two
        act_two = jax.nn.relu(pre_two).astype(jnp.bfloat16)
        proj_out = jnp.dot(act_two, w_three, preferred_element_type=jnp.float32)
        normed_out, inv_out = norm_forward(proj_out, total_rows)
        embed_pair = normed_out.astype(jnp.bfloat16)
        corr_part = lax.dot_general(embed_pair[0], embed_pair[1], FIRST_DIMS, preferred_element_type=jnp.float32)
        corr_mat = lax.psum(corr_part, "data") / total_rows
        feat_index = jnp.arange(corr_mat.shape[0])
        diag_mask = feat_index[:, None] == feat_index[None, :]
        diag_gap = 1.0 - corr_mat
        loss_total = jnp.sum(jnp.where(diag_mask, diag_gap * diag_gap, lam_off * corr_mat * corr_mat))
        grad_corr = jnp.where(diag_mask, -2.0 * diag_gap, 2.0 * lam_off * corr_mat)
        grad_scaled = (grad_corr / total_rows).astype(jnp.bfloat16)
        grad_embed_a = lax.dot_general(embed_pair[1], grad_scaled, (((1,), (1,)), ((), ())),
                                       preferred_element_type=jnp.float32)
        grad_embed_b = jnp.dot(embed_pair[0], grad_scaled, preferred_element_type=jnp.float32)
        grad_embed = jnp.stack([grad_embed_a, grad_embed_b])
        grad_proj = norm_backward(grad_embed, normed_out, inv_out, total_rows)[0].astype(jnp.bfloat16)
        grad_w_three = lax.psum_scatter(
            lax.dot_general(act_two, grad_proj, ROW_DIMS, preferred_element_type=jnp.float32),
            "data", scatter_dimension=0, tiled=True)
        grad_act_two = lax.dot_general(grad_proj, w_three, LAST_DIMS, preferred_element_type=jnp.float32)
        grad_pre_two = jnp.where(pre_two > 0, grad_act_two, 0.0)
        grad_hidden_two, sums_two = norm_backward(grad_pre_two, normed_two, inv_two, total_rows)
        grad_hidden_two = (gain_two * grad_hidden_two).astype(jnp.bfloat16)
        grad_w_two = lax.psum_scatter(
            lax.dot_general(act_one, grad_hidden_two, ROW_DIMS, preferred_element_type=jnp.float32),
            "data", scatter_dimension=0, tiled=True)
        grad_act_one = lax.dot_general(grad_hidden_two, w_two, LAST_DIMS, preferred_element_type=jnp.float32)
        grad_pre_one = jnp.where(pre_one > 0, grad_act_one, 0.0)
        grad_hidden_one, sums_one = norm_backward(grad_pre_one, normed_one, inv_one, total_rows)
        grad_hidden_one = (gain_one * grad_hidden_one).astype(jnp.bfloat16).reshape(2 * rows_dev, -1)
        grad_w_one = lax.psum_scatter(
            lax.dot_general(feat_rows, grad_hidden_one, FIRST_DIMS, preferred_element_type=jnp.float32),
            "data", scatter_dimension=0, tiled=True)
        return (loss_total, grad_w_one, grad_w_two, grad_w_three,
                jnp.sum(sums_one[1], axis=0), jnp.sum(sums_one[0], axis=0),
                jnp.sum(sums_two[1], axis=0), jnp.sum(sums_two[0], axis=0))

    row_spec = P("data", None)
    whole_mat = P(None, None)
    whole_vec = P(None)
    return jax.shard_map(
        local_step, mesh=mesh,
        in_specs=(row_spec, row_spec, whole_mat, whole_mat, whole_mat,
                  whole_vec, whole_vec, whole_vec, whole_vec, P()),
        out_specs=(P(), row_spec, row_spec, row_spec, whole_vec, whole_vec, whole_vec, whole_vec),
        check_vma=False)
```

profile of v0, /device:TPU:0, one launch (start us, length us, event | category | flops | bytes accessed | tf_op | source)
XLA Modules:
  0.0 781.1 jit_solution(17475903548031546953)
XLA Ops:
  7.2 0.0 copy-start
  7.2 0.0 all-reduce.2.cloned.1.call-start
  7.2 1.2 constant_dynamic-update-slice_fusion.1
  8.4 0.0 copy-start.9
  8.5 0.0 copy-start.11
  8.5 1.1 constant_dynamic-update-slice_fusion
  9.6 0.0 copy-done
  9.6 5.6 bitcast_reduce_fusion
  15.2 25.2 %psum.49 = f32[2,2,2048]{2,1,0:T(2,128)S(1)} all-reduce(f32[2,2,2048]{2,1,0:T(2,128)S(1)} %pad_maximum_fusion.1), channel_id=1, replica_groups=mesh['data'=8] {'data'}, use_global_device_ids=true, to_apply=%region_2.0 | all-reduce | flops 8192 | bytes 65536 | tf_op jit(solution)/shard_map/psum | solution.py:14
  40.5 0.0 copy-done.9
  40.5 0.0 copy-done.11
  40.5 0.0 copy-start.8
  40.5 0.0 copy-start.10
  40.5 15.8 %fusion.35 = (f32[2,2048]{1,0:T(2,128)S(1)}, f32[2,2048]{1,0:T(2,128)S(1)}, f32[2,512,2048]{2,1,0:T(8,128)}) fusion(bf16[2048,2048]{1,0:T(8,128)(2,1)} %param.13, f32[1024,2048]{1,0:T(8,128)} %get-tuple-element.30, f32[2048]{0:T(1024)S(1)} %copy-done.11, f32[2,2048]{1,0:T(2,128)S(1)} %fusion.30, f32[2,2048]{1,0:T(2,128)S(1)} %fusion.31, f32[2048]{0:T(1024)S(1)} %copy-done.9), kind=kOutput, calls=%fused_computation.84 | convolution fusion | flops 8608800768 | bytes 25247744 | tf_op jit(solution)/shard_map/dot_general | solution.py:37
  56.4 23.2 %psum.50 = f32[2,2,2048]{2,1,0:T(2,128)S(1)} all-reduce(f32[2,2,2048]{2,1,0:T(2,128)S(1)} %pad_maximum_fusion.2), channel_id=1, replica_groups=mesh['data'=8] {'data'}, use_global_device_ids=true, to_apply=%region_5.6 | all-reduce | flops 8192 | bytes 65536 | tf_op jit(solution)/shard_map/psum | solution.py:14
  79.6 0.0 copy-done.8
  79.6 0.0 copy-done.10
  79.6 15.8 %fusion.34 = (f32[2,2048]{1,0:T(2,128)S(1)}, f32[2,2048]{1,0:T(2,128)S(1)}, f32[2,512,2048]{2,1,0:T(8,128)}) fusion(bf16[2048,2048]{1,0:T(8,128)(2,1)} %param.14, f32[2,512,2048]{2,1,0:T(8,128)} %get-tuple-element.31, f32[2048]{0:T(1024)S(1)} %copy-done.10, f32[2,2048]{1,0:T(2,128)S(1)} %fusion.25, f32[2,2048]{1,0:T(2,128)S(1)} %fusion.26, ...), kind=kOutput, calls=%fused_computation.83 | convolution fusion | flops 8608800768 | bytes 25247744 | tf_op jit(solution)/shard_map/dot_general | solution.py:41
  95.4 24.4 %psum.51 = f32[2,2,2048]{2,1,0:T(2,128)S(1)} all-reduce(f32[2,2,2048]{2,1,0:T(2,128)S(1)} %pad_maximum_fusion.3), channel_id=1, replica_groups=mesh['data'=8] {'data'}, use_global_device_ids=true, to_apply=%region_8.9 | all-reduce | flops 8192 | bytes 65536 | tf_op jit(solution)/shard_map/psum | solution.py:14
  119.9 4.6 fusion.10
  124.5 0.0 copy-start.6
  124.5 1.9 copy-done.6
  126.4 8.1 %fusion.16 = f32[2048,2048]{1,0:T(8,128)} fusion(bf16[2,512,2048]{2,1,0:T(8,128)(2,1)S(1)} %fusion.10), kind=kOutput, calls=%fused_computation.41 | convolution fusion | flops 4294967296 | bytes 20971520 | tf_op jit(solution)/shard_map/dot_general | solution.py:44
  134.5 0.0 all-reduce.2.cloned.1.call-update
  134.5 0.0 reduce-scatter.4.cloned.1.call-start
  135.2 206.5 %all-reduce.2.cloned.1.call-done = f32[2048,2048]{1,0:T(8,128)} async-done(((f32[2048,2048]{1,0:T(8,128)}), f32[2048,2048]{1,0:T(8,128)}) %all-reduce.2.cloned.1.call-update) | async-done | bytes 16777232 | tf_op jit(solution)/shard_map/psum | solution.py:45
  341.7 10.1 %convolution_bitcast_fusion.3 = f32[1,512,2048]{2,1,0:T(8,128)S(1)} fusion(bf16[2,512,2048]{2,1,0:T(8,128)(2,1)} %copy-done.6, f32[2048,2048]{1,0:T(8,128)} %all-reduce.2.cloned.1.call-done, f32[]{:T(128)S(6)} %mul.190), kind=kOutput, calls=%fused_computation.38 | convolution fusion | flops 4328521728 | bytes 23068676 | tf_op jit(solution)/shard_map/dot_general | solution.py:52
  351.8 0.0 copy-done.7
  351.8 0.0 copy-start.2
  351.8 0.0 slice-start.1
  351.8 10.8 %convolution_bitcast_fusion.2 = f32[1,512,2048]{2,1,0:T(8,128)S(1)} fusion(bf16[2,512,2048]{2,1,0:T(8,128)(2,1)S(1)} %copy-done.7, f32[2048,2048]{1,0:T(8,128)} %all-reduce.2.cloned.1.call-done, f32[]{:T(128)S(6)} %mul.190), kind=kOutput, calls=%fused_computation.37 | convolution fusion | flops 4328521728 | bytes 23068676 | tf_op jit(solution)/shard_map/dot_general | solution.py:54
  362.6 0.0 copy-done.2
  362.7 0.0 slice-done
  362.7 0.0 slice-done.1
  362.7 0.0 copy-start.3
  362.7 2.3 fusion.11
  365.0 0.0 copy-done.3
  365.0 33.6 %psum.53 = f32[2,2,2048]{2,1,0:T(2,128)S(1)} all-reduce(f32[2,2,2048]{2,1,0:T(2,128)S(1)} %pad_maximum_fusion.4), channel_id=1, replica_groups=mesh['data'=8] {'data'}, use_global_device_ids=true, to_apply=%region_13.14 | all-reduce | flops 8192 | bytes 65536 | tf_op jit(solution)/shard_map/psum | solution.py:21
  398.7 7.1 multiply_convert_fusion.3
  405.7 0.0 copy-start.4
  405.7 17.4 %fusion.33 = (f32[2,2048]{1,0:T(2,128)S(1)}, f32[2,2048]{1,0:T(2,128)S(1)}, f32[2,512,2048]{2,1,0:T(8,128)}) fusion(f32[2,2048]{1,0:T(2,128)S(1)} %fusion.25, f32[2,512,2048]{2,1,0:T(8,128)} %get-tuple-element.31, f32[2,2048]{1,0:T(2,128)S(1)} %fusion.26, bf16[2,512,2048]{2,1,0:T(8,128)(2,1)S(1)} %multiply_convert_fusion.3, bf16[2048,2048]{1,0:T(8,128)(2,1)} %param.14, ...), kind=kOutput, calls=%fused_computation.82 | convolution fusion | flops 8608800768 | bytes 29442048 | tf_op jit(solution)/shard_map/dot_general | solution.py:60
  423.1 0.0 copy-done.4
  423.2 24.1 %psum.54 = f32[2,2,2048]{2,1,0:T(2,128)S(1)} all-reduce(f32[2,2,2048]{2,1,0:T(2,128)S(1)} %pad_maximum_fusion.5), channel_id=1, replica_groups=mesh['data'=8] {'data'}, use_global_device_ids=true, to_apply=%region_16.17 | all-reduce | flops 8192 | bytes 65536 | tf_op jit(solution)/shard_map/psum | solution.py:21
  447.3 0.6 slice_reduce_fusion.3
  448.0 7.1 multiply_convert_fusion.2
  455.1 0.0 copy-start.5
  455.1 17.4 %fusion.32 = (f32[2,2048]{1,0:T(2,128)S(1)}, f32[2,2048]{1,0:T(2,128)S(1)}, f32[2,512,2048]{2,1,0:T(8,128)}) fusion(f32[2,2048]{1,0:T(2,128)S(1)} %fusion.30, f32[2,2048]{1,0:T(2,128)S(1)} %fusion.31, f32[1024,2048]{1,0:T(8,128)} %get-tuple-element.30, bf16[2,512,2048]{2,1,0:T(8,128)(2,1)S(1)} %multiply_convert_fusion.2, bf16[2048,2048]{1,0:T(8,128)(2,1)} %param.13, ...), kind=kOutput, calls=%fused_computation.81 | convolution fusion | flops 8608800768 | bytes 29442048 | tf_op jit(solution)/shard_map/dot_general | solution.py:67
  472.5 0.0 copy-done.5
  472.5 23.2 %psum.55 = f32[2,2,2048]{2,1,0:T(2,128)S(1)} all-reduce(f32[2,2,2048]{2,1,0:T(2,128)S(1)} %pad_maximum_fusion.6), channel_id=1, replica_groups=mesh['data'=8] {'data'}, use_global_device_ids=true, to_apply=%region_19.20 | all-reduce | flops 8192 | bytes 65536 | tf_op jit(solution)/shard_map/psum | solution.py:21
  495.8 0.6 slice_reduce_fusion.1
  496.4 7.1 multiply_convert_fusion.1
  503.5 4.4 fusion.36
  507.9 0.0 reduce-scatter.4.cloned.1.call-update
  508.0 0.3 reduce-scatter.8.cloned.1.call-start
  508.2 15.9 %convolution_bitcast_fusion = f32[2048,2048]{1,0:T(8,128)} fusion(bf16[2,512,2048]{2,1,0:T(8,128)(2,1)} %copy-done.4, f32[2,512,2048]{2,1,0:T(8,128)} %get-tuple-element.31, f32[2048]{0:T(1024)S(1)} %copy-done.10, f32[2,2048]{1,0:T(2,128)S(1)} %fusion.25, f32[2,2048]{1,0:T(2,128)S(1)} %fusion.26, f32[2048]{0:T(1024)S(1)} %copy-done.8), kind=kOutput, calls=%fused_computation.3 | convolution fusion | flops 8602517504 | bytes 29409280 | tf_op jit(solution)/shard_map/dot_general | solution.py:58
  524.1 0.0 reduce-scatter.8.cloned.1.call-update
  524.2 0.0 reduce-scatter.6.cloned.1.call-start
  524.2 15.9 %convolution_bitcast_fusion.1 = f32[2048,2048]{1,0:T(8,128)} fusion(bf16[2,512,2048]{2,1,0:T(8,128)(2,1)} %copy-done.5, f32[1024,2048]{1,0:T(8,128)} %get-tuple-element.30, f32[2048]{0:T(1024)S(1)} %copy-done.11, f32[2,2048]{1,0:T(2,128)S(1)} %fusion.30, f32[2,2048]{1,0:T(2,128)S(1)} %fusion.31, f32[2048]{0:T(1024)S(1)} %copy-done.9), kind=kOutput, calls=%fused_computation.4 | convolution fusion | flops 8602517504 | bytes 29409280 | tf_op jit(solution)/shard_map/dot_general | solution.py:65
  540.1 0.0 reduce-scatter.6.cloned.1.call-update
  540.1 0.0 copy-start.1
  540.1 8.9 %select_reduce_fusion = f32[]{:T(128)} fusion(f32[2048,2048]{1,0:T(8,128)} %all-reduce.2.cloned.1.call-done, f32[]{:T(128)S(6)} %mul.184), kind=kLoop, calls=%fused_computation.1 | loop fusion | flops 33554432 | bytes 16777224 | tf_op jit(solution)/shard_map/reduce_sum | solution.py:49
  549.0 3.2 reduce-scatter.4.cloned.1.call-done
  552.3 111.1 %reduce-scatter.8.cloned.1.call-done = f32[256,2048]{1,0:T(8,128)} async-done(((f32[2048,2048]{1,0:T(8,128)}), f32[256,2048]{1,0:T(8,128)}) %reduce-scatter.8.cloned.1.call-update) | async-done | bytes 2097168 | tf_op jit(solution)/shard_map/reduce_scatter | solution.py:57
  663.3 110.9 %reduce-scatter.6.cloned.1.call-done = f32[256,2048]{1,0:T(8,128)} async-done(((f32[2048,2048]{1,0:T(8,128)}), f32[256,2048]{1,0:T(8,128)}) %reduce-scatter.6.cloned.1.call-update) | async-done | bytes 2097168 | tf_op jit(solution)/shard_map/reduce_scatter | solution.py:64
  (17 shorter events, 0.2 us)
Async XLA Ops:
  7.2 2.4 copy-start
  7.2 334.6 %all-reduce.2.cloned.1.call-start = ((), (), s32[]{:S(2)}) async-start(), calls=%async_computation.3 | async-start | bytes 33554432 | tf_op jit(solution)/shard_map/psum | solution.py:45
  8.4 32.0 %copy-start.9 = (f32[2048]{0:T(1024)S(1)}, f32[2048]{0:T(1024)}, u32[]{:S(2)}) copy-start(f32[2048]{0:T(1024)} %param.15) | copy-start | bytes 24580
  8.5 32.0 %copy-start.11 = (f32[2048]{0:T(1024)S(1)}, f32[2048]{0:T(1024)}, u32[]{:S(2)}) copy-start(f32[2048]{0:T(1024)} %param.16) | copy-start | bytes 24580
  40.5 39.1 %copy-start.8 = (f32[2048]{0:T(1024)S(1)}, f32[2048]{0:T(1024)}, u32[]{:S(2)}) copy-start(f32[2048]{0:T(1024)} %param.17) | copy-start | bytes 24580
  40.5 39.1 %copy-start.10 = (f32[2048]{0:T(1024)S(1)}, f32[2048]{0:T(1024)}, u32[]{:S(2)}) copy-start(f32[2048]{0:T(1024)} %param.18) | copy-start | bytes 24580
  124.5 1.9 copy-start.6
  134.5 417.7 %reduce-scatter.4.cloned.1.call-start = ((), (), s32[]{:S(2)}) async-start(), calls=%async_computation.4 | async-start | bytes 4718592 | tf_op jit(solution)/shard_map/reduce_scatter | solution.py:71
  341.7 10.1 %copy-start.7 = (bf16[2,512,2048]{2,1,0:T(8,128)(2,1)S(1)}, bf16[2,512,2048]{2,1,0:T(8,128)(2,1)}, u32[]{:S(2)}) copy-start(bf16[2,512,2048]{2,1,0:T(8,128)(2,1)} %copy-done.6) | copy-start | bytes 12582916
  341.7 20.9 %slice-start = ((s8[8388608]{0:T(1024)(128)(4,1)}), s8[4194304]{0:T(1024)(128)(4,1)S(1)}, s32[]{:S(2)}) async-start(s8[8388608]{0:T(1024)(128)(4,1)} %bitcast.127), calls=%async_computation.7 | async-start | bytes 8388608
  351.8 10.8 %copy-start.2 = (f32[1,512,2048]{2,1,0:T(8,128)}, f32[1,512,2048]{2,1,0:T(8,128)S(1)}, u32[]{:S(2)}) copy-start(f32[1,512,2048]{2,1,0:T(8,128)S(1)} %convolution_bitcast_fusion.3) | copy-start | bytes 12582916
  351.8 10.8 %slice-start.1 = ((s8[8388608]{0:T(1024)(128)(4,1)}), s8[4194304]{0:T(1024)(128)(4,1)S(1)}, s32[]{:S(2)}) async-start(s8[8388608]{0:T(1024)(128)(4,1)} %bitcast.127), calls=%async_computation.8 | async-start | bytes 8388608
  362.7 2.3 copy-start.3
  405.7 17.4 %copy-start.4 = (bf16[2,512,2048]{2,1,0:T(8,128)(2,1)}, bf16[2,512,2048]{2,1,0:T(8,128)(2,1)S(1)}, u32[]{:S(2)}) copy-start(bf16[2,512,2048]{2,1,0:T(8,128)(2,1)S(1)} %multiply_convert_fusion.3) | copy-start | bytes 12582916
  455.1 17.4 %copy-start.5 = (bf16[2,512,2048]{2,1,0:T(8,128)(2,1)}, bf16[2,512,2048]{2,1,0:T(8,128)(2,1)S(1)}, u32[]{:S(2)}) copy-start(bf16[2,512,2048]{2,1,0:T(8,128)(2,1)S(1)} %multiply_convert_fusion.2) | copy-start | bytes 12582916
  508.0 155.4 %reduce-scatter.8.cloned.1.call-start = ((), (), s32[]{:S(2)}) async-start(), calls=%async_computation.6 | async-start | bytes 18874368 | tf_op jit(solution)/shard_map/reduce_scatter | solution.py:57
  524.2 250.1 %reduce-scatter.6.cloned.1.call-start = ((), (), s32[]{:S(2)}) async-start(), calls=%async_computation.5 | async-start | bytes 18874368 | tf_op jit(solution)/shard_map/reduce_scatter | solution.py:64
  540.1 234.1 %copy-start.1 = (bf16[512,2048]{1,0:T(8,128)(2,1)S(1)}, bf16[512,2048]{1,0:T(8,128)(2,1)}, u32[]{:S(2)}) copy-start(bf16[512,2048]{1,0:T(8,128)(2,1)} %param.12) | copy-start | bytes 6291460
Sparse Core Ops, SparseCore 0:
  134.7 207.0 all-reduce.1
  508.1 44.1 reduce-scatter.3
  556.3 106.9 reduce-scatter.7
  667.2 106.9 reduce-scatter.5
where the time goes:
time: 790 us; the launch traced here: 781 us
  waiting for transfers between devices  432 us (55%)
  blocking collectives  154 us (19%)
  matrix products  137 us (17%)
  other arithmetic  38.6 us (5%)
  between operations  15.2 us (2%)
    psum x1, waiting for transfers between devices, local_step(): corr_mat = lax.psum(corr_part, 'data') / total_rows  206 us
    reduce_scatter x1, waiting for transfers between devices, local_step(): lax.psum_scatter(lax.dot_general(act_two, grad_proj, ROW_DIMS, preferred_...  111 us
    reduce_scatter x1, waiting for transfers between devices, local_step(): lax.psum_scatter(lax.dot_general(act_one, grad_hidden_two, ROW_DIMS, pref...  111 us
    psum x3, blocking collectives, norm_backward(): lax.psum(jnp.stack([jnp.sum(grad_out, axis=1), jnp.sum(grad_out * normed,...  81 us
    psum x3, blocking collectives, norm_forward(): col_sums = lax.psum(col_sums, 'data')  72.8 us
    dot_general x1, matrix products, local_step(): lax.dot_general(grad_proj, w_three, LAST_DIMS, preferred_element_type=jnp...  17.4 us
    dot_general x1, matrix products, local_step(): lax.dot_general(grad_hidden_two, w_two, LAST_DIMS, preferred_element_type...  17.4 us
    dot_general x1, matrix products, local_step(): lax.dot_general(act_two, grad_proj, ROW_DIMS, preferred_element_type=jnp....  15.9 us
  transfers between devices with their start and end apart: 4, of which 4 were waited for; matrix products, arithmetic and copies ran while one was open for 5% of the time, Pallas kernels for 0%

commit v1 on v0

v1 whole, which is shorter than its diff:
```python
import functools

import jax
import jax.numpy as jnp
from jax import lax
from jax.experimental import pallas as pl
from jax.experimental.pallas import tpu as pltpu
from jax.sharding import PartitionSpec as P

NORM_EPS = 1e-5
MESH = pl.DeviceIdType.MESH
DEVICES = 8
OWN, PAIR, XN, XP, YN, YP, DG, DP = range(DEVICES)
FAR_FIRST = (DG, DP, XN, XP, YN, YP, PAIR)
ORDER = (OWN, XN, DG, YN)
TWO = range(2)
TILE = 256
TILES = 8
WEIGHTS = 3
GAIN, SHIFT, INV, MEAN, VEC_ROWS = 0, 1, 2, 4, 6
VMEM_BYTES = 67043328
TURN_LEFT = (((0,), (0,)), ((), ()))
TURN_RIGHT = (((1,), (1,)), ((), ()))
F32, BF16 = jnp.float32, jnp.bfloat16
DMA = pltpu.SemaphoreType.DMA


def dot(left, right, dims=None):
    if dims is None:
        return jnp.dot(left, right, preferred_element_type=F32)
    return lax.dot_general(left, right, dims, preferred_element_type=F32)


def span(index, size):
    return pl.ds(pl.multiple_of(index * size, size), size)


def cols(n):
    return span(n, TILE)


def row(ref, r, c):
    return ref[r:r + 1, c]


def remote(src, dst, send, recv, mask):
    return pltpu.make_async_remote_copy(src_ref=src, dst_ref=dst, send_sem=send, recv_sem=recv,
                                        device_id=(lax.axis_index("data") ^ mask,), device_id_type=MESH)


def greet():
    for mask in FAR_FIRST:
        pl.semaphore_signal(pltpu.get_barrier_semaphore(), inc=1, device_id=(lax.axis_index("data") ^ mask,),
                            device_id_type=MESH)


def all_entered():
    pl.semaphore_wait(pltpu.get_barrier_semaphore(), len(FAR_FIRST))


def column_sums(ref, lead, r, c, first, second):
    ref[lead + (slice(r, r + 1), c)] = jnp.sum(first, axis=0, keepdims=True)
    ref[lead + (slice(r + 1, r + 2), c)] = jnp.sum(second, axis=0, keepdims=True)


def exchange(mine, slots, send, recv):
    me = lax.axis_index("data")

    def copy(e, mask):
        return remote(mine.at[e], slots.at[e, me], send.at[e, mask], recv.at[e, mask], mask)

    def start(e):
        for mask in FAR_FIRST:
            copy(e, mask).start()
        slots[e, me] = mine[e]

    def take(e):
        for mask in FAR_FIRST:
            copy(e, mask).wait()
        return functools.reduce(jnp.add, [slots[e, k] for k in range(DEVICES)])
    return start, take


def run(copies):
    for copy in copies:
        copy.start()
    return copies


def finish_all(copies):
    for copy in copies:
        copy.wait()


def backward_kernel(rows_total, dz, x2, x2_pair, x1, x1_pair, h_a, h_b, w3, w2, u2, u1, vec2, vec1,
                    gw3, gw2, gw1, sums2, sums1,
                    d, pd, xt, hv, hturn, ht, dpre, wbuf, nbuf, acc3, acc2, acc1, near3, near2, near1, far3, far2, far1,
                    mine, slots, load_sem, pair_send, pair_recv, hop_send, hop_recv, far_send, far_recv,
                    sum_send, sum_recv, h_send, h_recv, out_sem, w_sem, n_sem, free_sem):
    me = lax.axis_index("data")
    rows = d.shape[0]
    half = rows // 2
    greet()
    all_entered()
    send_sums, take_sums = exchange(mine, slots, sum_send, sum_recv)

    def pair_copy(src, n):
        return remote(src.at[:, cols(n)], pd.at[:, cols(n)], pair_send.at[n], pair_recv.at[n], PAIR)

    def both_colours(body):
        def step(i, carry):
            for colour in TWO:
                body(colour * (TILES // 2) + i, colour)
            return carry
        lax.fori_loop(0, TILES // 2, step, 0)

    class Product:
        def __init__(self, w, lhs, acc, near, far, out):
            self.w, self.lhs, self.acc, self.near, self.far, self.out = w, lhs, acc, near, far, out
            self.blk = out.shape[0]

        def block(self, j, count=1):
            return pl.ds(j * self.blk, count * self.blk)

        def first_hop(self, n, colour):
            return remote(self.acc.at[n, self.block(1 + colour, 2)], self.near.at[n],
                          hop_send.at[self.w, n], hop_recv.at[self.w, n], YN if colour else XN)

        def second_hop(self, n, colour):
            return remote(self.acc.at[n, self.block(1 if colour else 3)], self.far.at[n],
                          far_send.at[self.w, n], far_recv.at[self.w, n], XN if colour else YN)

        def out_copy(self, n):
            return pltpu.make_async_copy(self.acc.at[n, self.block(0)], self.out.at[:, cols(n)], out_sem.at[self.w, n])

        def compute(self, src):
            def body(n, colour):
                pair_copy(src, n).wait()
                self.acc[n] = self.lhs(0, d[:, cols(n)]) + self.lhs(1, pd[:, cols(n)])
                self.first_hop(n, colour).start()
            both_colours(body)

        def relay(self):
            def body(n, colour):
                onward, own = self.block(1 if colour else 3), self.block(0)
                self.first_hop(n, colour).wait_recv()
                self.acc[n, onward] = self.acc[n, onward] + self.near[n, self.block(1 - colour)]
                self.second_hop(n, colour).start()
                self.acc[n, own] = self.acc[n, own] + self.near[n, self.block(colour)]
            both_colours(body)

        def finish(self):
            def body(n, colour):
                own = self.block(0)
                self.second_hop(n, colour).wait_recv()
                self.acc[n, own] = self.acc[n, own] + self.far[n]
                self.out_copy(n).start()
            both_colours(body)

        def drain(self):
            def body(n, colour):
                self.first_hop(n, colour).wait_send()
                self.second_hop(n, colour).wait_send()
                self.out_copy(n).wait()
            both_colours(body)

    def w_tile(src, i):
        return pltpu.make_async_copy(src.at[cols(i)], wbuf.at[i % 2], w_sem.at[i % 2])

    def n_tile(src, i):
        return pltpu.make_async_copy(src.at[:, cols(i)], nbuf.at[i % 2], n_sem.at[i % 2])

    def tiles(streams, body):
        run([s(0) for s in streams])

        def step(i, carry):
            @pl.when(i < TILES - 1)
            def _():
                run([s(i + 1) for s in streams])
            finish_all([s(i) for s in streams])
            body(i, cols(i))
            return carry
        lax.fori_loop(0, TILES, step, 0)

    def normed_tile(i, c, v, vec):
        return (nbuf[i % 2, span(v, half), :] - row(vec, MEAN + v, c)) * row(vec, INV + v, c)

    def back_product(w_src, n_src, vec, which):
        def body(i, c):
            for v in TWO:
                grad = dot(d[span(v, half), :], wbuf[i % 2], TURN_RIGHT)
                normed = normed_tile(i, c, v, vec)
                grad = jnp.where(row(vec, GAIN, c) * normed + row(vec, SHIFT, c) > 0, grad, 0.0)
                dpre[span(v, half), c] = grad
                column_sums(mine, (which,), 2 * v, c, grad, grad * normed)
        tiles([functools.partial(w_tile, w_src), functools.partial(n_tile, n_src)], body)

    def norm_grad(n_src, vec, sums):
        def body(i, c):
            for v in TWO:
                part = span(v, half)
                mean, slope = row(sums, 2 * v, c) / rows_total, row(sums, 2 * v + 1, c) / rows_total
                grad = row(vec, GAIN, c) * row(vec, INV + v, c) * (
                    dpre[part, c] - (mean + normed_tile(i, c, v, vec) * slope))
                d[part, c] = grad.astype(BF16)
            pair_copy(d, i).start()
        tiles([functools.partial(n_tile, n_src)], body)

    def load(src, dst, k):
        return pltpu.make_async_copy(src, dst, load_sem.at[k])

    both_colours(lambda n, colour: pair_copy(dz, n).start())
    blk3, blk1 = gw3.shape[0], gw1.shape[0]

    def operand(src, pair):
        return [load(pair, xt.at[span(1, rows)], len(ORDER))] + [
            load(src.at[:, span(me ^ mask, blk3)], xt.at[span(0, rows), pl.ds(j * blk3, blk3)], j)
            for j, mask in enumerate(ORDER)]

    def lhs_x(k, right):
        return dot(xt[span(k, rows), :], right, TURN_LEFT)

    def lhs_h(k, right):
        return dot(ht[:, span(k, rows)], right)

    prod3 = Product(0, lhs_x, acc3, near3, far3, gw3)
    prod2 = Product(1, lhs_x, acc2, near2, far2, gw2)
    prod1 = Product(2, lhs_h, acc1, near1, far1, gw1)
    finish_all(run([load(dz, d, len(ORDER) + 1)] + operand(x2, x2_pair)))
    prod3.compute(dz)
    second = run(operand(x1, x1_pair))
    views = list(enumerate((h_a, h_b)))
    own_h = run([load(src, hv.at[span(v, half)], len(ORDER) + 1 + v) for v, src in views])
    pair_h = run([remote(src, hv.at[span(2 + v, half)], h_send.at[v], h_recv.at[v], PAIR) for v, src in views])
    back_product(w3, u2, vec2, 0)
    send_sums(0)
    prod3.relay()
    sums2[...] = take_sums(0)
    norm_grad(u2, vec2, sums2)
    finish_all(second)
    prod2.compute(d)
    pl.semaphore_signal(free_sem, inc=1, device_id=(me ^ PAIR,), device_id_type=MESH)
    back_product(w2, u1, vec1, 1)
    send_sums(1)
    finish_all(own_h + pair_h)
    for k in range(2 * len(TWO)):
        hturn[:, span(k, half)] = hv[span(k, half), :].T
    for j, mask in enumerate(ORDER):
        ht[span(j, blk1), :] = hturn[span(me ^ mask, blk1), :]
    prod3.finish()
    prod2.relay()
    sums1[...] = take_sums(1)
    pl.semaphore_wait(free_sem, 1)
    norm_grad(u1, vec1, sums1)
    prod1.compute(d)
    prod1.relay()
    prod2.finish()
    prod1.finish()
    for product in (prod3, prod2, prod1):
        product.drain()


ANYWHERE, ON_CHIP = pl.BlockSpec(memory_space=pl.ANY), pl.BlockSpec(memory_space=pltpu.VMEM)


def params(cid):
    return pltpu.CompilerParams(collective_id=cid, has_side_effects=True, vmem_limit_bytes=VMEM_BYTES)


def backward(rows_total, dz, *rest, cid):
    h_a = rest[4]
    rows, feats = dz.shape
    blk3, blk1 = feats // DEVICES, h_a.shape[1] // DEVICES
    groups = len(ORDER)
    blocks = (blk3, blk3, blk1)

    def per_weight(parts):
        return [pltpu.VMEM((TILES, parts * b, TILE), F32) for b in blocks]

    sums = jax.ShapeDtypeStruct((2 * len(TWO), feats), F32)
    return pl.pallas_call(
        functools.partial(backward_kernel, rows_total),
        out_shape=[jax.ShapeDtypeStruct((b, feats), F32) for b in blocks] + [sums, sums],
        in_specs=[ANYWHERE] * (len(rest) - 1) + [ON_CHIP] * 2,
        out_specs=[ANYWHERE] * WEIGHTS + [ON_CHIP] * 2,
        scratch_shapes=[pltpu.VMEM((rows, feats), BF16), pltpu.VMEM((rows, feats), BF16),
                        pltpu.VMEM((2 * rows, groups * blk3), BF16), pltpu.VMEM((2 * rows, h_a.shape[1]), BF16),
                        pltpu.VMEM((h_a.shape[1], 2 * rows), BF16), pltpu.VMEM((groups * blk1, 2 * rows), BF16),
                        pltpu.VMEM((rows, feats), F32),
                        pltpu.VMEM((2, TILE, feats), BF16), pltpu.VMEM((2, rows, TILE), F32)]
        + per_weight(groups) + per_weight(2) + per_weight(1)
        + [pltpu.VMEM((2,) + sums.shape, F32), pltpu.VMEM((2, DEVICES) + sums.shape, F32), DMA((DEVICES,))]
        + [DMA((TILES,))] * 2 + [DMA((WEIGHTS, TILES))] * 4 + [DMA((2, DEVICES))] * 2 + [DMA((2,))] * 2
        + [DMA((WEIGHTS, TILES))] + [DMA((2,))] * 2 + [pltpu.SemaphoreType.REGULAR],
        compiler_params=params(cid),
        name="backward",
    )(dz, *rest)


def forward_kernel(rows_total, lam, h_a, h_b, w1, w2, w3, gain1, shift1, gain2, shift2,
                   loss, u1, u2, x1, x2, x1_pair, x2_pair, dz, vec1, vec2,
                   hv, ubuf, vbuf, w2buf, w3buf, xbuf, zh, za, zb, corr, mine, slots, vec3, loss_mine, loss_slots,
                   load_sem, store_sem, pair_send, pair_recv, sum_send, sum_recv, za_send, za_recv, zb_send, zb_recv,
                   g_send, g_recv, loss_send, loss_recv, dz_sem):
    me = lax.axis_index("data")
    half = hv.shape[0] // 2
    feats = w2buf.shape[0]
    rblk, cblk = za.shape[2], zb.shape[2]
    greet()

    def load(src, dst, k):
        return pltpu.make_async_copy(src, dst, load_sem.at[k])

    w1_view = w3buf.at[pl.ds(0, w1.shape[0])]
    loads = run([load(h_a, hv.at[span(0, half)], 0), load(h_b, hv.at[span(1, half)], 1), load(w1, w1_view, 2)])
    all_entered()
    send_sums, take_sums = exchange(mine, slots, sum_send, sum_recv)
    send_loss, take_loss = exchange(loss_mine, loss_slots, loss_send, loss_recv)

    def each_tile(body):
        def step(n, carry):
            body(n, cols(n))
            return carry
        lax.fori_loop(0, TILES, step, 0)

    def take_vectors(e, v, vec):
        total = take_sums(e) / rows_total
        mean = total[:1]
        vec[pl.ds(MEAN + v, 1), :] = mean
        vec[pl.ds(INV + v, 1), :] = lax.rsqrt(total[1:] - mean * mean + NORM_EPS)

    def layer(e, v, left, weight, out):
        part = span(v, half)

        def body(n, c):
            value = dot(left[part, :], weight[:, c])
            out[part, c] = value
            column_sums(mine, (e,), 0, c, value, value * value)
        each_tile(body)
        send_sums(e)

    def normed_tile(values, v, c, vec):
        return (values[span(v, half), c] - row(vec, MEAN + v, c)) * row(vec, INV + v, c)

    def activate(v, values, vec):
        def body(n, c):
            pre = row(vec, GAIN, c) * normed_tile(values, v, c, vec) + row(vec, SHIFT, c)
            xbuf[span(v, half), c] = jnp.maximum(pre, 0.0).astype(BF16)
        each_tile(body)

    def store(src, dst, k):
        return pltpu.make_async_copy(src, dst, store_sem.at[k])

    def keep_rows(dst, pair, index):
        blk = feats // DEVICES
        return run([store(xbuf, dst, 2)] + [
            remote(xbuf.at[:, span(me ^ mask ^ PAIR, blk)], pair.at[:, pl.ds(j * blk, blk)],
                   pair_send.at[index, j], pair_recv.at[index, j], PAIR) for j, mask in enumerate(ORDER)])

    for vec, gain, shift in ((vec1, gain1, shift1), (vec2, gain2, shift2)):
        vec[pl.ds(GAIN, 1), :] = gain[...]
        vec[pl.ds(SHIFT, 1), :] = shift[...]
    finish_all(loads)
    load_w2 = load(w2, w2buf, 0)
    load_w2.start()
    for v in TWO:
        layer(v, v, hv, w1_view, ubuf)
    load_w3 = load(w3, w3buf, 2)
    store_u1 = store(ubuf, u1, 0)
    run([load_w3, store_u1])
    kept = []
    for v in TWO:
        take_vectors(v, v, vec1)
        activate(v, ubuf, vec1)
        if v:
            kept = keep_rows(x1, x1_pair, 0)
        else:
            load_w2.wait()
        layer(2 + v, v, xbuf, w2buf, vbuf)
    store_u2 = store(vbuf, u2, 1)
    store_u2.start()
    finish_all([store_u1, load_w3] + kept)
    for v in TWO:
        take_vectors(2 + v, v, vec2)
        activate(v, vbuf, vec2)
        if v:
            kept = keep_rows(x2, x2_pair, 1)
        layer(4 + v, v, xbuf, w3buf, ubuf)

    def embed(v):
        take_vectors(4 + v, v, vec3)

        def body(n, c):
            zh[span(v, half), c] = normed_tile(ubuf, v, c, vec3).astype(BF16)
        each_tile(body)

    def row_index(mask):
        dev = me ^ mask
        return dev // 4 * 2 + dev % 2

    def row_block(mask):
        return span(row_index(mask), rblk)

    def col_block(mask):
        return span((me ^ mask) // 2 % 2, cblk)

    quarter = half // 2
    started = []

    def go(copy):
        copy.start()
        started.append(copy)

    def za_direct(mask):
        return remote(zh.at[span(0, half), row_block(mask)], za.at[me], za_send.at[mask], za_recv.at[mask], mask)

    def za_relay(origin):
        slot = za.at[me ^ origin]
        return remote(slot, slot, za_send.at[origin ^ XN], za_recv.at[origin ^ XN], XN)

    def zb_slot(origin, k):
        return zb.at[me ^ origin, span(k, quarter)]

    def zb_direct(mask, k):
        return remote(zh.at[span(2 + k, quarter), col_block(mask)], zb_slot(OWN, k),
                      zb_send.at[mask, k], zb_recv.at[mask, k], mask)

    def zb_relay(origin, mask, k, send):
        return remote(zb_slot(origin, k), zb_slot(origin, k), zb_send.at[send, k], zb_recv.at[origin ^ mask, k], mask)

    def za_arrived(origin):
        slot = za.at[me ^ origin]
        remote(slot, slot, za_send.at[OWN], za_recv.at[origin], PAIR).wait_recv()

    def zb_arrived(origin, ks=TWO):
        for k in ks:
            zb_relay(origin, OWN, k, OWN).wait_recv()

    def accumulate(origin):
        corr[...] = corr[...] + dot(za[me ^ origin], zb[me ^ origin], TURN_LEFT)

    embed(0)
    for mask in (YN, XN, YP, XP, PAIR):
        go(za_direct(mask))
    embed(1)
    for k in TWO:
        for mask in (XN, YN, PAIR):
            go(zb_direct(mask, k))
    corr[...] = dot(zh[span(0, half), row_block(OWN)], zh[span(1, half), col_block(OWN)], TURN_LEFT)
    za_arrived(PAIR)
    zb_arrived(PAIR)
    accumulate(PAIR)
    for origin in (YN, YP):
        za_arrived(origin)
        go(za_relay(origin))
    for k in TWO:
        zb_arrived(XN, (k,))
        go(zb_relay(XN, YN, k, XP))
        go(zb_relay(XN, PAIR, k, YP))
        zb_arrived(YN, (k,))
        go(zb_relay(YN, PAIR, k, DG))
    za_arrived(XN)
    accumulate(XN)
    accumulate(YN)
    za_arrived(XP)
    for origin in (XP, YP):
        zb_arrived(origin)
        accumulate(origin)
    for k in TWO:
        zb_arrived(DG, (k,))
        go(zb_relay(DG, PAIR, k, DP))
    za_arrived(DG)
    accumulate(DG)
    za_arrived(DP)
    zb_arrived(DP)
    accumulate(DP)

    lam_off = lam[0]
    row_start, col_start = row_index(OWN) * rblk, me // 2 % 2 * cblk

    def grad_body(n, total):
        value = corr[:, cols(n)] / rows_total
        row_ids = row_start + lax.broadcasted_iota(jnp.int32, value.shape, 0)
        col_ids = col_start + n * TILE + lax.broadcasted_iota(jnp.int32, value.shape, 1)
        diag = row_ids == col_ids
        gap = 1.0 - value
        terms = jnp.where(diag, gap * gap, lam_off * value * value)
        grad = jnp.where(diag, -2.0 * gap, 2.0 * lam_off * value) / rows_total
        w2buf[row_block(OWN), pl.ds(pl.multiple_of(col_start + n * TILE, TILE), TILE)] = grad.astype(BF16)
        return total + jnp.sum(terms, axis=0, keepdims=True)
    loss_row = lax.fori_loop(0, cblk // TILE, grad_body, jnp.zeros((1, TILE), F32))

    pieces = g_send.shape[1]
    piece = rblk // pieces

    def g_slot(origin, k):
        return w2buf.at[span(row_index(origin) * pieces + k, piece), col_block(origin)]

    def g_copy(origin, mask, k, send):
        return remote(g_slot(origin, k), g_slot(origin, k), g_send.at[send, k], g_recv.at[origin ^ mask, k], mask)

    def g_arrived(origin, ks):
        for k in ks:
            g_copy(origin, OWN, k, OWN).wait_recv()

    def contribute(origin, k, count):
        part = span(row_index(origin) * (pieces // count) + k // count, count * piece)
        block = w2buf[part, col_block(origin)]
        first = dot(zh[span(1, half), col_block(origin)], block, TURN_RIGHT)
        where_a, where_b = (span(0, half), part), (span(1, half), col_block(origin))
        vbuf[where_a] = vbuf[where_a] + first if origin & XN else first
        second = dot(zh[span(0, half), part], block)
        vbuf[where_b] = second if origin in (OWN, XN) and not k else vbuf[where_b] + second

    every = range(pieces)
    even, odd = every[::2], every[1::2]
    for k, j in zip((*even, *odd), (*odd, *even)):
        go(g_copy(OWN, XN, k, PAIR))
        go(g_copy(OWN, YN, j, XN))
    for k in every:
        go(g_copy(OWN, PAIR, k, XP))
    loss_mine[0] = jnp.broadcast_to(jnp.sum(loss_row, axis=1, keepdims=True), loss_mine.shape[1:])
    send_loss(0)
    store_u2.wait()
    contribute(OWN, 0, pieces)
    g_arrived(PAIR, every)
    contribute(PAIR, 0, pieces)
    for k, j in zip(even, odd):
        g_arrived(XN, (k,))
        go(g_copy(XN, YN, k, YN))
        go(g_copy(XN, PAIR, k, YP))
        g_arrived(YN, (j,))
        go(g_copy(YN, XN, j, YN))
        go(g_copy(YN, PAIR, j, DG))
    for k, j in zip(odd, even):
        g_arrived(XN, (k,))
        go(g_copy(XN, PAIR, k, YP))
        g_arrived(YN, (j,))
        go(g_copy(YN, PAIR, j, DG))
    contribute(YN, 0, pieces)
    contribute(XN, 0, pieces)
    for origin in (YP, XP):
        g_arrived(origin, every)
        contribute(origin, 0, pieces)
    for k in even:
        now = (k, k + 1)
        for j in now:
            g_arrived(DG, (j,))
            go(g_copy(DG, PAIR, j, DP))
        contribute(DG, k, len(now))
        g_arrived(DP, now)
        contribute(DP, k, len(now))

    def sums_body(n, c):
        for v in TWO:
            grad = vbuf[span(v, half), c]
            column_sums(mine, (DG + v,), 0, c, grad, grad * normed_tile(ubuf, v, c, vec3))
    each_tile(sums_body)
    for v in TWO:
        send_sums(DG + v)
    finish_all(kept)
    loss[...] = take_loss(0)
    for v in TWO:
        mine[DG + v] = take_sums(DG + v) / rows_total

    def dz_copy(n):
        return pltpu.make_async_copy(xbuf.at[:, cols(n)], dz.at[:, cols(n)], dz_sem.at[n])

    def dz_body(n, c):
        for v in TWO:
            sums = mine[DG + v, :, c]
            grad = row(vec3, INV + v, c) * (
                vbuf[span(v, half), c] - (sums[:1] + normed_tile(ubuf, v, c, vec3) * sums[1:]))
            xbuf[span(v, half), c] = grad.astype(BF16)
        dz_copy(n).start()
    each_tile(dz_body)
    for copy in started:
        copy.wait_send()
    each_tile(lambda n, c: dz_copy(n).wait())


def forward(rows_total, lam, h_a, h_b, w1, w2, w3, *vectors, cid):
    half, depth = h_a.shape
    feats = w2.shape[0]
    full, pair, vec = (2 * half, feats), (2 * half, feats // 2), (VEC_ROWS, feats)
    small = (DEVICES, 128)
    outs = [(small, F32), (full, F32), (full, F32), (full, BF16), (full, BF16), (pair, BF16), (pair, BF16), (full, BF16),
            (vec, F32), (vec, F32)]
    scratch = [((2 * half, depth), BF16), (full, F32), (full, F32), ((feats, feats), BF16), ((feats, feats), BF16),
               (full, BF16), (full, BF16), ((DEVICES, half, feats // 4), BF16), ((DEVICES, half, feats // 2), BF16),
               ((feats // 4, feats // 2), F32), ((DEVICES, 2, feats), F32), ((DEVICES, DEVICES, 2, feats), F32),
               (vec, F32), ((1,) + small, F32), ((1, DEVICES) + small, F32)]
    return pl.pallas_call(
        functools.partial(forward_kernel, rows_total),
        out_shape=[jax.ShapeDtypeStruct(*out) for out in outs],
        in_specs=[pl.BlockSpec(memory_space=pltpu.SMEM)] + [ANYWHERE] * 5 + [ON_CHIP] * len(vectors),
        out_specs=[ON_CHIP] + [ANYWHERE] * (len(outs) - WEIGHTS) + [ON_CHIP] * 2,
        scratch_shapes=[pltpu.VMEM(*item) for item in scratch]
        + [DMA((WEIGHTS,))] * 2 + [DMA((2, len(ORDER)))] * 2 + [DMA((DEVICES, DEVICES))] * 2 + [DMA((DEVICES,))] * 2
        + [DMA((DEVICES, 2))] * 2 + [DMA((DEVICES, 4))] * 2 + [DMA((1, DEVICES))] * 2 + [DMA((TILES,))],
        compiler_params=params(cid),
        name="forward",
    )(lam, h_a, h_b, w1, w2, w3, *vectors)


def emit_kernel(gw3, gw2, gw1, sums2, sums1, out3, out2, out1, gain1, shift1, gain2, shift2, buf, in_sem, out_sem):
    step = gw1.shape[0]
    pieces = [(src, dst, k) for src, dst in ((gw3, out3), (gw2, out2), (gw1, out1)) for k in range(src.shape[0] // step)]
    ins = run([pltpu.make_async_copy(src.at[span(k, step)], buf.at[i], in_sem.at[i])
               for i, (src, dst, k) in enumerate(pieces)])
    outs = [pltpu.make_async_copy(buf.at[i], dst.at[span(k, step)], out_sem.at[i])
            for i, (src, dst, k) in enumerate(pieces)]
    for sums, gain, shift in ((sums1, gain1, shift1), (sums2, gain2, shift2)):
        both = sums[:2, :] + sums[2:, :]
        shift[...] = both[:1]
        gain[...] = both[1:]
    for before, after in zip(ins, outs):
        before.wait()
        after.start()
    finish_all(outs)


def emit(gw3, gw2, gw1, sums2, sums1):
    weights = (gw3, gw2, gw1)
    step, feats = gw1.shape
    count = sum(g.shape[0] for g in weights) // step
    return pl.pallas_call(
        emit_kernel,
        out_shape=[jax.ShapeDtypeStruct(g.shape, F32) for g in weights] + [jax.ShapeDtypeStruct((1, feats), F32)] * 4,
        in_specs=[ANYWHERE] * WEIGHTS + [ON_CHIP] * 2,
        out_specs=[ANYWHERE] * WEIGHTS + [ON_CHIP] * 4,
        scratch_shapes=[pltpu.VMEM((count, step, feats), F32)] + [DMA((count,))] * 2,
        name="emit",
    )(*weights, sums2, sums1)


def solution(mesh):
    shards = mesh.shape["data"]

    def local_step(h_a, h_b, w_one, w_two, w_three, gain_one, shift_one, gain_two, shift_two, lam_off):
        total_rows = h_a.shape[0] * shards
        loss, u1, u2, x1, x2, x1_pair, x2_pair, dz, vec1, vec2 = forward(
            total_rows, lam_off.reshape(1), h_a, h_b, w_one, w_two, w_three,
            *[v[None] for v in (gain_one, shift_one, gain_two, shift_two)], cid=0)
        grads = backward(total_rows, dz, x2, x2_pair, x1, x1_pair, h_a, h_b, w_three, w_two, u2, u1, vec2, vec1, cid=1)
        grad_w_three, grad_w_two, grad_w_one, *rest = emit(*grads)
        return (loss[0, 0], grad_w_one, grad_w_two, grad_w_three, *[v[0] for v in rest])

    row_spec = P("data", None)
    whole_mat = P(None, None)
    whole_vec = P(None)
    return jax.shard_map(
        local_step, mesh=mesh,
        in_specs=(row_spec, row_spec, whole_mat, whole_mat, whole_mat,
                  whole_vec, whole_vec, whole_vec, whole_vec, P()),
        out_specs=(P(), row_spec, row_spec, row_spec, whole_vec, whole_vec, whole_vec, whole_vec),
        check_vma=False)
```

time: 790 us -> 347 us (0.44)
  waiting for transfers between devices: 432 us -> 0 us
  Pallas kernels: 0 us -> 343 us
  blocking collectives: 154 us -> 0 us
  matrix products: 137 us -> 0 us
  other arithmetic: 38.6 us -> 0 us
  between operations: 15.2 us -> 1.48 us
    pallas_call x0 -> x3, Pallas kernels: none -> 343 us  [the longest x1 173 us: backward(): pl.pallas_call(functools.partial(backward_kernel, rows_total), out_shape=...]
    reduce_scatter x3 -> x0, waiting for transfers between devices: 225 us -> none  [the longest x1 111 us: local_step(): lax.psum_scatter(lax.dot_general(act_two, grad_proj, ROW_DIMS, preferred_...]
    psum x1 -> x0, waiting for transfers between devices: 206 us -> none  [local_step(): corr_mat = lax.psum(corr_part, 'data') / total_rows]
    psum x6 -> x0, blocking collectives: 154 us -> none  [the longest x3 81 us: norm_backward(): lax.psum(jnp.stack([jnp.sum(grad_out, axis=1), jnp.sum(grad_out * normed,...]
    dot_general x11 -> x0, matrix products: 137 us -> none  [the longest x1 17.4 us: local_step(): lax.dot_general(grad_proj, w_three, LAST_DIMS, preferred_element_type=jnp...]
    convert_element_type x4 -> x0, other arithmetic: 25.9 us -> none  [the longest x1 7.14 us: local_step(): grad_hidden_two = (gain_two * grad_hidden_two).astype(jnp.bfloat16)]
    reduce_sum x4 -> x0, other arithmetic: 12.5 us -> none  [the longest x1 8.89 us: local_step(): jnp.sum(jnp.where(diag_mask, diag_gap * diag_gap, lam_off * corr_mat * co...]
  transfers between devices with their start and end apart: 4 -> 0, of which waited for: 4 -> 0; matrix products, arithmetic and copies ran while one was open for 5% -> 0% of each run, Pallas kernels for 0% -> 0%
where the time goes in v1:
time: 347 us; the launch traced here: 346 us
  Pallas kernels  343 us (99%)
    pallas_call x1, Pallas kernels, backward(): pl.pallas_call(functools.partial(backward_kernel, rows_total), out_shape=...  173 us
    pallas_call x1, Pallas kernels, forward(): pl.pallas_call(functools.partial(forward_kernel, rows_total), out_shape=[...  165 us

profile of v1, /device:TPU:0, one launch (start us, length us, event | category | flops | bytes accessed | tf_op | source)
XLA Modules:
  0.0 345.6 jit_solution(15622065095945768864)
XLA Ops:
  1.3 164.7 %forward.1 = (f32[8,128]{1,0:T(8,128)}, f32[1024,2048]{1,0:T(8,128)}, f32[1024,2048]{1,0:T(8,128)}, bf16[1024,2048]{1,0:T(8,128)(2,1)}, bf16[1024,2048]{1,0:T(8,...) custom-call(f32[1]{0:T(128)} %bitcast.10.lam, ...), custom_call_target="tpu_custom_call" | custom-call | tf_op jit(solution)/shard_map/forward/pallas_call | solution.py:593
  166.0 1.2 slice.3
  167.2 172.7 %backward.1 = (f32[256,2048]{1,0:T(8,128)}, f32[256,2048]{1,0:T(8,128)}, f32[64,2048]{1,0:T(8,128)}, f32[4,2048]{1,0:T(4,128)}, f32[4,2048]{1,0:T(4,128)}) custom-call(bf16[1024,2048]{1,0:T(8,128)(2,1)} %get-tuple-element.31.dz, bf16[1024,2048]{1,0:T(8,128)(2,1)} %get-tuple-element.32.x2, bf16[1024,1024]{1,0:T(8,128)(2,1)} %get-tuple-element.33.x2_pair, ...), custom_call_target="tpu_custom_call" | custom-call | tf_op jit(solution)/shard_map/backward/pallas_call | solution.py:281
  339.9 5.5 %emit.1 = (f32[256,2048]{1,0:T(8,128)}, f32[256,2048]{1,0:T(8,128)}, f32[64,2048]{1,0:T(8,128)}, f32[1,2048]{1,0:T(1,128)}, f32[1,2048]{1,0:T(1,128)}, /*index=5*/f32[1,2048]{1,0:T(1,128)}, f32[1,2048]{1,0:T(1,128)}) custom-call(f32[256,2048]{1,0:T(8,128)} %get-tuple-element.40.gw3, f32[256,2048]{1,0:T(8,128)} %get-tuple-element.41.gw2, ...), custom_call_target="tpu_custom_call" | custom-call | tf_op jit(solution)/shard_map/emit/pallas_call | solution.py:627

commit v2 on v1

--- a/solution.py
+++ b/solution.py
@@ -81,6 +81,41 @@
     return start, take
 
 
+def exchange_halves(mine, mate, chips, whole, send, recv):
+    me = lax.axis_index("data")
+    width = mate.shape[-1]
+    core, chip = me % 2, me // 2
+    others = (DG, XN, YN)
+
+    def pair_copy(e):
+        return remote(mine.at[e, :, span(1 - core, width)], mate.at[e], send.at[e, OWN], recv.at[e, OWN], PAIR)
+
+    def chip_copy(e, mask):
+        return remote(chips.at[e, chip], chips.at[e, chip], send.at[e, mask], recv.at[e, mask], mask)
+
+    def share(e):
+        half = whole.at[e, :, span(core, width)]
+        return remote(half, half, send.at[e, PAIR], recv.at[e, PAIR], PAIR)
+
+    def start(e):
+        pair_copy(e).start()
+
+    def middle(e):
+        pair_copy(e).wait()
+        chips[e, chip] = mine[e, :, span(core, width)] + mate[e]
+        for mask in others:
+            chip_copy(e, mask).start()
+
+    def take(e):
+        for mask in others:
+            chip_copy(e, mask).wait()
+        whole[e, :, span(core, width)] = functools.reduce(jnp.add, [chips[e, k] for k in range(DEVICES // 2)])
+        share(e).start()
+        share(e).wait()
+        return whole[e]
+    return start, middle, take
+
+
 def run(copies):
     for copy in copies:
         copy.start()
@@ -92,20 +127,19 @@
         copy.wait()
 
 
-def backward_kernel(rows_total, dz, x2, x2_pair, x1, x1_pair, h_a, h_b, w3, w2, u2, u1, vec2, vec1,
+def backward_kernel(rows_total, dz, dz_pair, x2, x2_pair, x1, x1_pair, h_a, h_b, w3, w2, u2, u1, vec2, vec1,
                     gw3, gw2, gw1, sums2, sums1,
                     d, pd, xt, hv, hturn, ht, dpre, wbuf, nbuf, acc3, acc2, acc1, near3, near2, near1, far3, far2, far1,
-                    mine, slots, load_sem, pair_send, pair_recv, hop_send, hop_recv, far_send, far_recv,
+                    mine, mate, chips, whole, load_sem, tile_sem, pair_send, pair_recv, hop_send, hop_recv, far_send, far_recv,
                     sum_send, sum_recv, h_send, h_recv, out_sem, w_sem, n_sem, free_sem):
     me = lax.axis_index("data")
     rows = d.shape[0]
     half = rows // 2
     greet()
-    all_entered()
-    send_sums, take_sums = exchange(mine, slots, sum_send, sum_recv)
-
-    def pair_copy(src, n):
-        return remote(src.at[:, cols(n)], pd.at[:, cols(n)], pair_send.at[n], pair_recv.at[n], PAIR)
+    send_sums, pass_sums, take_sums = exchange_halves(mine, mate, chips, whole, sum_send, sum_recv)
+
+    def pair_copy(n):
+        return remote(d.at[:, cols(n)], pd.at[:, cols(n)], pair_send.at[n], pair_recv.at[n], PAIR)
 
     def both_colours(body):
         def step(i, carry):
@@ -133,11 +167,17 @@
         def out_copy(self, n):
             return pltpu.make_async_copy(self.acc.at[n, self.block(0)], self.out.at[:, cols(n)], out_sem.at[self.w, n])
 
-        def compute(self, src):
+        def fill(self, n, part):
+            self.acc[n, part] = self.lhs(0, part, d[:, cols(n)]) + self.lhs(1, part, pd[:, cols(n)])
+
+        def compute(self, parts, arrive, send):
             def body(n, colour):
-                pair_copy(src, n).wait()
-                self.acc[n] = self.lhs(0, d[:, cols(n)]) + self.lhs(1, pd[:, cols(n)])
-                self.first_hop(n, colour).start()
+                if arrive:
+                    arrive(n)
+                for j, count in parts[colour]:
+                    self.fill(n, self.block(j, count))
+                if send:
+                    self.first_hop(n, colour).start()
             both_colours(body)
 
         def relay(self):
@@ -203,13 +243,16 @@
                 grad = row(vec, GAIN, c) * row(vec, INV + v, c) * (
                     dpre[part, c] - (mean + normed_tile(i, c, v, vec) * slope))
                 d[part, c] = grad.astype(BF16)
-            pair_copy(d, i).start()
+            pair_copy(i).start()
         tiles([functools.partial(n_tile, n_src)], body)
 
     def load(src, dst, k):
         return pltpu.make_async_copy(src, dst, load_sem.at[k])
 
-    both_colours(lambda n, colour: pair_copy(dz, n).start())
+    def dz_tiles(n):
+        return [pltpu.make_async_copy(src.at[:, cols(n)], dst.at[:, cols(n)], tile_sem.at[k, n])
+                for k, (src, dst) in enumerate(((dz, d), (dz_pair, pd)))]
+
     blk3, blk1 = gw3.shape[0], gw1.shape[0]
 
     def operand(src, pair):
@@ -217,28 +260,34 @@
             load(src.at[:, span(me ^ mask, blk3)], xt.at[span(0, rows), pl.ds(j * blk3, blk3)], j)
             for j, mask in enumerate(ORDER)]
 
-    def lhs_x(k, right):
-        return dot(xt[span(k, rows), :], right, TURN_LEFT)
-
-    def lhs_h(k, right):
-        return dot(ht[:, span(k, rows)], right)
+    def lhs_x(k, part, right):
+        return dot(xt[span(k, rows), part], right, TURN_LEFT)
+
+    def lhs_h(k, part, right):
+        return dot(ht[part, span(k, rows)], right)
 
     prod3 = Product(0, lhs_x, acc3, near3, far3, gw3)
     prod2 = Product(1, lhs_x, acc2, near2, far2, gw2)
     prod1 = Product(2, lhs_h, acc1, near1, far1, gw1)
-    finish_all(run([load(dz, d, len(ORDER) + 1)] + operand(x2, x2_pair)))
-    prod3.compute(dz)
+    first = run(operand(x2, x2_pair))
+    both_colours(lambda n, colour: run(dz_tiles(n)) and None)
+    all_entered()
+    finish_all(first)
+    everything = ([(0, len(ORDER))],) * 2
+    prod3.compute(([(1, 2)], [(2, 2)]), lambda n: finish_all(dz_tiles(n)), True)
+    back_product(w3, u2, vec2, 0)
+    send_sums(0)
+    prod3.compute(([(0, 1), (3, 1)], [(0, 2)]), None, False)
+    pass_sums(0)
     second = run(operand(x1, x1_pair))
     views = list(enumerate((h_a, h_b)))
     own_h = run([load(src, hv.at[span(v, half)], len(ORDER) + 1 + v) for v, src in views])
     pair_h = run([remote(src, hv.at[span(2 + v, half)], h_send.at[v], h_recv.at[v], PAIR) for v, src in views])
-    back_product(w3, u2, vec2, 0)
-    send_sums(0)
     prod3.relay()
     sums2[...] = take_sums(0)
     norm_grad(u2, vec2, sums2)
     finish_all(second)
-    prod2.compute(d)
+    prod2.compute(everything, lambda n: pair_copy(n).wait(), True)
     pl.semaphore_signal(free_sem, inc=1, device_id=(me ^ PAIR,), device_id_type=MESH)
     back_product(w2, u1, vec1, 1)
     send_sums(1)
@@ -247,12 +296,13 @@
         hturn[:, span(k, half)] = hv[span(k, half), :].T
     for j, mask in enumerate(ORDER):
         ht[span(j, blk1), :] = hturn[span(me ^ mask, blk1), :]
+    pass_sums(1)
     prod3.finish()
     prod2.relay()
     sums1[...] = take_sums(1)
     pl.semaphore_wait(free_sem, 1)
     norm_grad(u1, vec1, sums1)
-    prod1.compute(d)
+    prod1.compute(everything, lambda n: pair_copy(n).wait(), True)
     prod1.relay()
     prod2.finish()
     prod1.finish()
@@ -261,6 +311,7 @@
 
 
 ANYWHERE, ON_CHIP = pl.BlockSpec(memory_space=pl.ANY), pl.BlockSpec(memory_space=pltpu.VMEM)
+SCALARS = pl.BlockSpec(memory_space=pltpu.SMEM)
 
 
 def params(cid):
@@ -268,7 +319,7 @@
 
 
 def backward(rows_total, dz, *rest, cid):
-    h_a = rest[4]
+    h_a = rest[5]
     rows, feats = dz.shape
     blk3, blk1 = feats // DEVICES, h_a.shape[1] // DEVICES
     groups = len(ORDER)
@@ -278,6 +329,7 @@
         return [pltpu.VMEM((TILES, parts * b, TILE), F32) for b in blocks]
 
     sums = jax.ShapeDtypeStruct((2 * len(TWO), feats), F32)
+    half_sums = (2 * len(TWO), feats // 2)
     return pl.pallas_call(
         functools.partial(backward_kernel, rows_total),
         out_shape=[jax.ShapeDtypeStruct((b, feats), F32) for b in blocks] + [sums, sums],
@@ -289,7 +341,9 @@
                         pltpu.VMEM((rows, feats), F32),
                         pltpu.VMEM((2, TILE, feats), BF16), pltpu.VMEM((2, rows, TILE), F32)]
         + per_weight(groups) + per_weight(2) + per_weight(1)
-        + [pltpu.VMEM((2,) + sums.shape, F32), pltpu.VMEM((2, DEVICES) + sums.shape, F32), DMA((DEVICES,))]
+        + [pltpu.VMEM(shape, F32) for shape in ((2,) + sums.shape, (2,) + half_sums, (2, DEVICES // 2) + half_sums,
+                                                (2,) + sums.shape)]
+        + [DMA((DEVICES,)), DMA((2, TILES))]
         + [DMA((TILES,))] * 2 + [DMA((WEIGHTS, TILES))] * 4 + [DMA((2, DEVICES))] * 2 + [DMA((2,))] * 2
         + [DMA((WEIGHTS, TILES))] + [DMA((2,))] * 2 + [pltpu.SemaphoreType.REGULAR],
         compiler_params=params(cid),
@@ -298,10 +352,10 @@
 
 
 def forward_kernel(rows_total, lam, h_a, h_b, w1, w2, w3, gain1, shift1, gain2, shift2,
-                   loss, u1, u2, x1, x2, x1_pair, x2_pair, dz, vec1, vec2,
+                   loss, u1, u2, x1, x2, x1_pair, x2_pair, dz, dz_pair, vec1, vec2,
                    hv, ubuf, vbuf, w2buf, w3buf, xbuf, zh, za, zb, corr, mine, slots, vec3, loss_mine, loss_slots,
                    load_sem, store_sem, pair_send, pair_recv, sum_send, sum_recv, za_send, za_recv, zb_send, zb_recv,
-                   g_send, g_recv, loss_send, loss_recv, dz_sem):
+                   g_send, g_recv, loss_send, loss_recv, dz_sem, dz_send, dz_recv):
     me = lax.axis_index("data")
     half = hv.shape[0] // 2
     feats = w2buf.shape[0]
@@ -563,8 +617,10 @@
     for v in TWO:
         mine[DG + v] = take_sums(DG + v) / rows_total
 
-    def dz_copy(n):
-        return pltpu.make_async_copy(xbuf.at[:, cols(n)], dz.at[:, cols(n)], dz_sem.at[n])
+    def dz_copies(n):
+        tile = xbuf.at[:, cols(n)]
+        return [remote(tile, dz_pair.at[:, cols(n)], dz_send.at[n], dz_recv.at[n], PAIR),
+                pltpu.make_async_copy(tile, dz.at[:, cols(n)], dz_sem.at[n])]
 
     def dz_body(n, c):
         for v in TWO:
@@ -572,11 +628,11 @@
             grad = row(vec3, INV + v, c) * (
                 vbuf[span(v, half), c] - (sums[:1] + normed_tile(ubuf, v, c, vec3) * sums[1:]))
             xbuf[span(v, half), c] = grad.astype(BF16)
-        dz_copy(n).start()
+        run(dz_copies(n))
     each_tile(dz_body)
     for copy in started:
         copy.wait_send()
-    each_tile(lambda n, c: dz_copy(n).wait())
+    each_tile(lambda n, c: finish_all(dz_copies(n)))
 
 
 def forward(rows_total, lam, h_a, h_b, w1, w2, w3, *vectors, cid):
@@ -584,7 +640,7 @@
     feats = w2.shape[0]
     full, pair, vec = (2 * half, feats), (2 * half, feats // 2), (VEC_ROWS, feats)
     small = (DEVICES, 128)
-    outs = [(small, F32), (full, F32), (full, F32), (full, BF16), (full, BF16), (pair, BF16), (pair, BF16), (full, BF16),
+    outs = [(small, F32), (full, F32), (full, F32), (full, BF16), (full, BF16), (pair, BF16), (pair, BF16), (full, BF16), (full, BF16),
             (vec, F32), (vec, F32)]
     scratch = [((2 * half, depth), BF16), (full, F32), (full, F32), ((feats, feats), BF16), ((feats, feats), BF16),
                (full, BF16), (full, BF16), ((DEVICES, half, feats // 4), BF16), ((DEVICES, half, feats // 2), BF16),
@@ -593,17 +649,17 @@
     return pl.pallas_call(
         functools.partial(forward_kernel, rows_total),
         out_shape=[jax.ShapeDtypeStruct(*out) for out in outs],
-        in_specs=[pl.BlockSpec(memory_space=pltpu.SMEM)] + [ANYWHERE] * 5 + [ON_CHIP] * len(vectors),
+        in_specs=[SCALARS] + [ANYWHERE] * 5 + [ON_CHIP] * len(vectors),
         out_specs=[ON_CHIP] + [ANYWHERE] * (len(outs) - WEIGHTS) + [ON_CHIP] * 2,
         scratch_shapes=[pltpu.VMEM(*item) for item in scratch]
         + [DMA((WEIGHTS,))] * 2 + [DMA((2, len(ORDER)))] * 2 + [DMA((DEVICES, DEVICES))] * 2 + [DMA((DEVICES,))] * 2
-        + [DMA((DEVICES, 2))] * 2 + [DMA((DEVICES, 4))] * 2 + [DMA((1, DEVICES))] * 2 + [DMA((TILES,))],
+        + [DMA((DEVICES, 2))] * 2 + [DMA((DEVICES, 4))] * 2 + [DMA((1, DEVICES))] * 2 + [DMA((TILES,))] * WEIGHTS,
         compiler_params=params(cid),
         name="forward",
     )(lam, h_a, h_b, w1, w2, w3, *vectors)
 
 
-def emit_kernel(gw3, gw2, gw1, sums2, sums1, out3, out2, out1, gain1, shift1, gain2, shift2, buf, in_sem, out_sem):
+def emit_kernel(gw3, gw2, gw1, sums2, sums1, loss, loss_out, out3, out2, out1, gain1, shift1, gain2, shift2, buf, in_sem, out_sem):
     step = gw1.shape[0]
     pieces = [(src, dst, k) for src, dst in ((gw3, out3), (gw2, out2), (gw1, out1)) for k in range(src.shape[0] // step)]
     ins = run([pltpu.make_async_copy(src.at[span(k, step)], buf.at[i], in_sem.at[i])
@@ -614,24 +670,26 @@
         both = sums[:2, :] + sums[2:, :]
         shift[...] = both[:1]
         gain[...] = both[1:]
+    loss_out[0, 0] = loss[0, 0]
     for before, after in zip(ins, outs):
         before.wait()
         after.start()
     finish_all(outs)
 
 
-def emit(gw3, gw2, gw1, sums2, sums1):
+def emit(gw3, gw2, gw1, sums2, sums1, loss):
     weights = (gw3, gw2, gw1)
     step, feats = gw1.shape
     count = sum(g.shape[0] for g in weights) // step
     return pl.pallas_call(
         emit_kernel,
-        out_shape=[jax.ShapeDtypeStruct(g.shape, F32) for g in weights] + [jax.ShapeDtypeStruct((1, feats), F32)] * 4,
-        in_specs=[ANYWHERE] * WEIGHTS + [ON_CHIP] * 2,
-        out_specs=[ANYWHERE] * WEIGHTS + [ON_CHIP] * 4,
+        out_shape=[jax.ShapeDtypeStruct((1, 1), F32)] + [jax.ShapeDtypeStruct(g.shape, F32) for g in weights]
+        + [jax.ShapeDtypeStruct((1, feats), F32)] * 4,
+        in_specs=[ANYWHERE] * WEIGHTS + [ON_CHIP] * 2 + [SCALARS],
+        out_specs=[SCALARS] + [ANYWHERE] * WEIGHTS + [ON_CHIP] * 4,
         scratch_shapes=[pltpu.VMEM((count, step, feats), F32)] + [DMA((count,))] * 2,
         name="emit",
-    )(*weights, sums2, sums1)
+    )(*weights, sums2, sums1, loss)
 
 
 def solution(mesh):
@@ -639,12 +697,13 @@
 
     def local_step(h_a, h_b, w_one, w_two, w_three, gain_one, shift_one, gain_two, shift_two, lam_off):
         total_rows = h_a.shape[0] * shards
-        loss, u1, u2, x1, x2, x1_pair, x2_pair, dz, vec1, vec2 = forward(
+        loss, u1, u2, x1, x2, x1_pair, x2_pair, dz, dz_pair, vec1, vec2 = forward(
             total_rows, lam_off.reshape(1), h_a, h_b, w_one, w_two, w_three,
             *[v[None] for v in (gain_one, shift_one, gain_two, shift_two)], cid=0)
-        grads = backward(total_rows, dz, x2, x2_pair, x1, x1_pair, h_a, h_b, w_three, w_two, u2, u1, vec2, vec1, cid=1)
-        grad_w_three, grad_w_two, grad_w_one, *rest = emit(*grads)
-        return (loss[0, 0], grad_w_one, grad_w_two, grad_w_three, *[v[0] for v in rest])
+        grads = backward(total_rows, dz, dz_pair, x2, x2_pair, x1, x1_pair, h_a, h_b, w_three, w_two, u2, u1, vec2, vec1,
+                         cid=1)
+        loss, grad_w_three, grad_w_two, grad_w_one, *rest = emit(*grads, loss)
+        return (loss.reshape(()), grad_w_one, grad_w_two, grad_w_three, *[v[0] for v in rest])
 
     row_spec = P("data", None)
     whole_mat = P(None, None)

time: 347 us -> 342 us (0.986)
  Pallas kernels: 343 us -> 339 us
    pallas_call x1, Pallas kernels: 173 us -> 165 us  [backward(): pl.pallas_call(functools.partial(backward_kernel, rows_total), out_shape=...]
    pallas_call x1, Pallas kernels: 165 us -> 169 us  [forward(): pl.pallas_call(functools.partial(forward_kernel, rows_total), out_shape=[...]
where the time goes in v2:
time: 342 us; the launch traced here: 341 us
  Pallas kernels  339 us (99%)
    pallas_call x1, Pallas kernels, forward(): pl.pallas_call(functools.partial(forward_kernel, rows_total), out_shape=[...  169 us
    pallas_call x1, Pallas kernels, backward(): pl.pallas_call(functools.partial(backward_kernel, rows_total), out_shape=...  165 us

profile of v2, /device:TPU:0, one launch (start us, length us, event | category | flops | bytes accessed | tf_op | source)
XLA Modules:
  0.0 340.8 jit_solution(14839654783688890656)
XLA Ops:
  1.3 169.2 %forward.1 = (f32[8,128]{1,0:T(8,128)}, f32[1024,2048]{1,0:T(8,128)}, f32[1024,2048]{1,0:T(8,128)}, bf16[1024,2048]{1,0:T(8,128)(2,1)}, bf16[1024,2048]{1,0:T(8,...) custom-call(f32[1]{0:T(128)} %bitcast.10.lam, ...), custom_call_target="tpu_custom_call" | custom-call | tf_op jit(solution)/shard_map/forward/pallas_call | solution.py:649
  170.5 164.5 %backward.1 = (f32[256,2048]{1,0:T(8,128)}, f32[256,2048]{1,0:T(8,128)}, f32[64,2048]{1,0:T(8,128)}, f32[4,2048]{1,0:T(4,128)}, f32[4,2048]{1,0:T(4,128)}) custom-call(bf16[1024,2048]{1,0:T(8,128)(2,1)} %get-tuple-element.32.dz, bf16[1024,2048]{1,0:T(8,128)(2,1)} %get-tuple-element.33.dz_pair, bf16[1024,2048]{1,0:T(8,128)(2,1)} %get-tuple-element.34.x2, ...), custom_call_target="tpu_custom_call" | custom-call | tf_op jit(solution)/shard_map/backward/pallas_call | solution.py:333
  335.0 5.6 %emit.1 = (f32[1,1]{1,0:T(1,128)}, f32[256,2048]{1,0:T(8,128)}, f32[256,2048]{1,0:T(8,128)}, f32[64,2048]{1,0:T(8,128)}, f32[1,2048]{1,0:T(1,128)}, /*index=5*/f...) custom-call(f32[256,2048]{1,0:T(8,128)} %get-tuple-element.42.gw3, f32[256,2048]{1,0:T(8,128)} %get-tuple-element.43.gw2, ...), custom_call_target="tpu_custom_call" | custom-call | tf_op jit(solution)/shard_map/emit/pallas_call | solution.py:684

commit v3 on v2

--- a/solution.py
+++ b/solution.py
@@ -138,8 +138,8 @@
     greet()
     send_sums, pass_sums, take_sums = exchange_halves(mine, mate, chips, whole, sum_send, sum_recv)
 
-    def pair_copy(n):
-        return remote(d.at[:, cols(n)], pd.at[:, cols(n)], pair_send.at[n], pair_recv.at[n], PAIR)
+    def pair_copy(n, src=d):
+        return remote(src.at[:, cols(n)], pd.at[:, cols(n)], pair_send.at[n], pair_recv.at[n], PAIR)
 
     def both_colours(body):
         def step(i, carry):
@@ -249,9 +249,15 @@
     def load(src, dst, k):
         return pltpu.make_async_copy(src, dst, load_sem.at[k])
 
-    def dz_tiles(n):
-        return [pltpu.make_async_copy(src.at[:, cols(n)], dst.at[:, cols(n)], tile_sem.at[k, n])
-                for k, (src, dst) in enumerate(((dz, d), (dz_pair, pd)))]
+    def dz_tile(n):
+        return pltpu.make_async_copy(dz.at[:, cols(n)], d.at[:, cols(n)], tile_sem.at[n])
+
+    heads = (0, TILES // 2)
+    passed = [pair_copy(n, dz) for i in range(1, TILES // 2) for n in (i, TILES // 2 + i)]
+
+    def dz_arrived(n):
+        dz_tile(n).wait()
+        pair_copy(n).wait_recv()
 
     blk3, blk1 = gw3.shape[0], gw1.shape[0]
 
@@ -270,14 +276,18 @@
     prod2 = Product(1, lhs_x, acc2, near2, far2, gw2)
     prod1 = Product(2, lhs_h, acc1, near1, far1, gw1)
     first = run(operand(x2, x2_pair))
-    both_colours(lambda n, colour: run(dz_tiles(n)) and None)
+    run([pltpu.make_async_copy(dz_pair.at[:, cols(k)], pd.at[:, cols(n)], pair_recv.at[n]) for k, n in enumerate(heads)])
+    both_colours(lambda n, colour: dz_tile(n).start())
     all_entered()
+    run(passed)
     finish_all(first)
     everything = ([(0, len(ORDER))],) * 2
-    prod3.compute(([(1, 2)], [(2, 2)]), lambda n: finish_all(dz_tiles(n)), True)
+    prod3.compute(([(1, 2)], [(2, 2)]), dz_arrived, True)
     back_product(w3, u2, vec2, 0)
     send_sums(0)
     prod3.compute(([(0, 1), (3, 1)], [(0, 2)]), None, False)
+    for copy in passed:
+        copy.wait_send()
     pass_sums(0)
     second = run(operand(x1, x1_pair))
     views = list(enumerate((h_a, h_b)))
@@ -343,7 +353,7 @@
         + per_weight(groups) + per_weight(2) + per_weight(1)
         + [pltpu.VMEM(shape, F32) for shape in ((2,) + sums.shape, (2,) + half_sums, (2, DEVICES // 2) + half_sums,
                                                 (2,) + sums.shape)]
-        + [DMA((DEVICES,)), DMA((2, TILES))]
+        + [DMA((DEVICES,)), DMA((TILES,))]
         + [DMA((TILES,))] * 2 + [DMA((WEIGHTS, TILES))] * 4 + [DMA((2, DEVICES))] * 2 + [DMA((2,))] * 2
         + [DMA((WEIGHTS, TILES))] + [DMA((2,))] * 2 + [pltpu.SemaphoreType.REGULAR],
         compiler_params=params(cid),
@@ -532,30 +542,39 @@
     lam_off = lam[0]
     row_start, col_start = row_index(OWN) * rblk, me // 2 % 2 * cblk
 
-    def grad_body(n, total):
-        value = corr[:, cols(n)] / rows_total
-        row_ids = row_start + lax.broadcasted_iota(jnp.int32, value.shape, 0)
-        col_ids = col_start + n * TILE + lax.broadcasted_iota(jnp.int32, value.shape, 1)
+    pieces = g_send.shape[1]
+    piece = rblk // pieces
+
+    def g_slot(origin, k):
+        return w2buf.at[span(row_index(origin) * pieces + k, piece), col_block(origin)]
+
+    def g_copy(origin, mask, k, send):
+        return remote(g_slot(origin, k), g_slot(origin, k), g_send.at[send, k], g_recv.at[origin ^ mask, k], mask)
+
+    def g_arrived(origin, ks):
+        for k in ks:
+            g_copy(origin, OWN, k, OWN).wait_recv()
+
+    def grad_piece(k):
+        value = corr[span(k, piece), :] / rows_total
+        row_ids = row_start + k * piece + lax.broadcasted_iota(jnp.int32, value.shape, 0)
+        col_ids = col_start + lax.broadcasted_iota(jnp.int32, value.shape, 1)
         diag = row_ids == col_ids
         gap = 1.0 - value
         terms = jnp.where(diag, gap * gap, lam_off * value * value)
         grad = jnp.where(diag, -2.0 * gap, 2.0 * lam_off * value) / rows_total
-        w2buf[row_block(OWN), pl.ds(pl.multiple_of(col_start + n * TILE, TILE), TILE)] = grad.astype(BF16)
-        return total + jnp.sum(terms, axis=0, keepdims=True)
-    loss_row = lax.fori_loop(0, cblk // TILE, grad_body, jnp.zeros((1, TILE), F32))
-
-    pieces = g_send.shape[1]
-    piece = rblk // pieces
-
-    def g_slot(origin, k):
-        return w2buf.at[span(row_index(origin) * pieces + k, piece), col_block(origin)]
-
-    def g_copy(origin, mask, k, send):
-        return remote(g_slot(origin, k), g_slot(origin, k), g_send.at[send, k], g_recv.at[origin ^ mask, k], mask)
-
-    def g_arrived(origin, ks):
-        for k in ks:
-            g_copy(origin, OWN, k, OWN).wait_recv()
+        w2buf[span(row_index(OWN) * pieces + k, piece), col_block(OWN)] = grad.astype(BF16)
+        return jnp.sum(terms, axis=0, keepdims=True)
+
+    every = range(pieces)
+    even, odd = every[::2], every[1::2]
+    loss_row = jnp.zeros((1, cblk), F32)
+    for k in every:
+        loss_row = loss_row + grad_piece(k)
+        go(g_copy(OWN, *((YN, k, XN) if k in odd else (XN, k, PAIR))))
+    for k, j in zip(odd, even):
+        go(g_copy(OWN, XN, k, PAIR))
+        go(g_copy(OWN, YN, j, XN))
 
     def contribute(origin, k, count):
         part = span(row_index(origin) * (pieces // count) + k // count, count * piece)
@@ -566,11 +585,6 @@
         second = dot(zh[span(0, half), part], block)
         vbuf[where_b] = second if origin in (OWN, XN) and not k else vbuf[where_b] + second
 
-    every = range(pieces)
-    even, odd = every[::2], every[1::2]
-    for k, j in zip((*even, *odd), (*odd, *even)):
-        go(g_copy(OWN, XN, k, PAIR))
-        go(g_copy(OWN, YN, j, XN))
     for k in every:
         go(g_copy(OWN, PAIR, k, XP))
     loss_mine[0] = jnp.broadcast_to(jnp.sum(loss_row, axis=1, keepdims=True), loss_mine.shape[1:])
@@ -596,6 +610,27 @@
     for origin in (YP, XP):
         g_arrived(origin, every)
         contribute(origin, 0, pieces)
+    def dz_columns(v, late):
+        first = me // 2 % 2 if v else me // 4
+        return span(1 - first if late else first, cblk)
+
+    def dz_sum_copy(v, late, mask):
+        e, c = DG + v, dz_columns(v, late)
+        k = DEVICES + v if late else e
+        return remote(mine.at[e, :, c], slots.at[e, me, :, c], sum_send.at[k, mask], sum_recv.at[k, mask], mask)
+
+    def dz_sums(late):
+        for v in TWO:
+            def body(t, carry, v=v):
+                start = dz_columns(v, late).start + t * TILE
+                c = pl.ds(pl.multiple_of(start, TILE), TILE)
+                grad = vbuf[span(v, half), c]
+                column_sums(mine, (DG + v,), 0, c, grad, grad * normed_tile(ubuf, v, c, vec3))
+                return carry
+            lax.fori_loop(0, cblk // TILE, body, 0)
+            run([dz_sum_copy(v, late, mask) for mask in FAR_FIRST])
+
+    dz_sums(False)
     for k in even:
         now = (k, k + 1)
         for j in now:
@@ -605,34 +640,42 @@
         g_arrived(DP, now)
         contribute(DP, k, len(now))
 
-    def sums_body(n, c):
-        for v in TWO:
-            grad = vbuf[span(v, half), c]
-            column_sums(mine, (DG + v,), 0, c, grad, grad * normed_tile(ubuf, v, c, vec3))
-    each_tile(sums_body)
-    for v in TWO:
-        send_sums(DG + v)
+    dz_sums(True)
     finish_all(kept)
     loss[...] = take_loss(0)
     for v in TWO:
-        mine[DG + v] = take_sums(DG + v) / rows_total
-
-    def dz_copies(n):
-        tile = xbuf.at[:, cols(n)]
-        return [remote(tile, dz_pair.at[:, cols(n)], dz_send.at[n], dz_recv.at[n], PAIR),
-                pltpu.make_async_copy(tile, dz.at[:, cols(n)], dz_sem.at[n])]
-
-    def dz_body(n, c):
+        slots[DG + v, me] = mine[DG + v]
+    for v in TWO:
+        finish_all([dz_sum_copy(v, late, mask) for late in (False, True) for mask in FAR_FIRST])
+        mine[DG + v] = functools.reduce(jnp.add, [slots[DG + v, k] for k in range(DEVICES)]) / rows_total
+
+    def dz_copy(n):
+        return pltpu.make_async_copy(xbuf.at[:, cols(n)], dz.at[:, cols(n)], dz_sem.at[n])
+
+    def dz_tile(n):
+        c = cols(n)
         for v in TWO:
             sums = mine[DG + v, :, c]
             grad = row(vec3, INV + v, c) * (
                 vbuf[span(v, half), c] - (sums[:1] + normed_tile(ubuf, v, c, vec3) * sums[1:]))
             xbuf[span(v, half), c] = grad.astype(BF16)
-        run(dz_copies(n))
-    each_tile(dz_body)
+        dz_copy(n).start()
+
+    heads = (0, TILES // 2)
+    for k, n in enumerate(heads):
+        dz_tile(n)
+        go(remote(xbuf.at[:, cols(n)], dz_pair.at[:, cols(k)], dz_send.at[k], dz_recv.at[k], PAIR))
+
+    def dz_body(i, carry):
+        for n in heads:
+            dz_tile(n + i)
+        return carry
+    lax.fori_loop(1, TILES // 2, dz_body, 0)
     for copy in started:
         copy.wait_send()
-    each_tile(lambda n, c: finish_all(dz_copies(n)))
+    for copy in started[-len(heads):]:
+        copy.wait_recv()
+    each_tile(lambda n, c: dz_copy(n).wait())
 
 
 def forward(rows_total, lam, h_a, h_b, w1, w2, w3, *vectors, cid):
@@ -640,7 +683,7 @@
     feats = w2.shape[0]
     full, pair, vec = (2 * half, feats), (2 * half, feats // 2), (VEC_ROWS, feats)
     small = (DEVICES, 128)
-    outs = [(small, F32), (full, F32), (full, F32), (full, BF16), (full, BF16), (pair, BF16), (pair, BF16), (full, BF16), (full, BF16),
+    outs = [(small, F32), (full, F32), (full, F32), (full, BF16), (full, BF16), (pair, BF16), (pair, BF16), (full, BF16), ((2 * half, 2 * TILE), BF16),
             (vec, F32), (vec, F32)]
     scratch = [((2 * half, depth), BF16), (full, F32), (full, F32), ((feats, feats), BF16), ((feats, feats), BF16),
                (full, BF16), (full, BF16), ((DEVICES, half, feats // 4), BF16), ((DEVICES, half, feats // 2), BF16),
@@ -652,8 +695,8 @@
         in_specs=[SCALARS] + [ANYWHERE] * 5 + [ON_CHIP] * len(vectors),
         out_specs=[ON_CHIP] + [ANYWHERE] * (len(outs) - WEIGHTS) + [ON_CHIP] * 2,
         scratch_shapes=[pltpu.VMEM(*item) for item in scratch]
-        + [DMA((WEIGHTS,))] * 2 + [DMA((2, len(ORDER)))] * 2 + [DMA((DEVICES, DEVICES))] * 2 + [DMA((DEVICES,))] * 2
-        + [DMA((DEVICES, 2))] * 2 + [DMA((DEVICES, 4))] * 2 + [DMA((1, DEVICES))] * 2 + [DMA((TILES,))] * WEIGHTS,
+        + [DMA((WEIGHTS,))] * 2 + [DMA((2, len(ORDER)))] * 2 + [DMA((DEVICES + 2, DEVICES))] * 2 + [DMA((DEVICES,))] * 2
+        + [DMA((DEVICES, 2))] * 2 + [DMA((DEVICES, 4))] * 2 + [DMA((1, DEVICES))] * 2 + [DMA((TILES,))] + [DMA((2,))] * 2,
         compiler_params=params(cid),
         name="forward",
     )(lam, h_a, h_b, w1, w2, w3, *vectors)

time: 342 us -> 334 us (0.977)
  Pallas kernels: 339 us -> 332 us
    pallas_call x1, Pallas kernels: 169 us -> 162 us  [forward(): pl.pallas_call(functools.partial(forward_kernel, rows_total), out_shape=[...]
where the time goes in v3:
time: 334 us; the launch traced here: 333 us
  Pallas kernels  332 us (99%)
    pallas_call x1, Pallas kernels, backward(): pl.pallas_call(functools.partial(backward_kernel, rows_total), out_shape=...  164 us
    pallas_call x1, Pallas kernels, forward(): pl.pallas_call(functools.partial(forward_kernel, rows_total), out_shape=[...  162 us

profile of v3, /device:TPU:0, one launch (start us, length us, event | category | flops | bytes accessed | tf_op | source)
XLA Modules:
  0.0 333.5 jit_solution(8688681217020570340)
XLA Ops:
  1.3 162.2 %forward.1 = (f32[8,128]{1,0:T(8,128)}, f32[1024,2048]{1,0:T(8,128)}, f32[1024,2048]{1,0:T(8,128)}, bf16[1024,2048]{1,0:T(8,128)(2,1)}, bf16[1024,2048]{1,0:T(8,...) custom-call(f32[1]{0:T(128)} %bitcast.10.lam, ...), custom_call_target="tpu_custom_call" | custom-call | tf_op jit(solution)/shard_map/forward/pallas_call | solution.py:692
  163.4 164.2 %backward.1 = (f32[256,2048]{1,0:T(8,128)}, f32[256,2048]{1,0:T(8,128)}, f32[64,2048]{1,0:T(8,128)}, f32[4,2048]{1,0:T(4,128)}, f32[4,2048]{1,0:T(4,128)}) custom-call(bf16[1024,2048]{1,0:T(8,128)(2,1)} %get-tuple-element.32.dz, bf16[1024,512]{1,0:T(8,128)(2,1)} %get-tuple-element.33.dz_pair, bf16[1024,2048]{1,0:T(8,128)(2,1)} %get-tuple-element.34.x2, ...), custom_call_target="tpu_custom_call" | custom-call | tf_op jit(solution)/shard_map/backward/pallas_call | solution.py:343
  327.6 5.6 %emit.1 = (f32[1,1]{1,0:T(1,128)}, f32[256,2048]{1,0:T(8,128)}, f32[256,2048]{1,0:T(8,128)}, f32[64,2048]{1,0:T(8,128)}, f32[1,2048]{1,0:T(1,128)}, /*index=5*/f...) custom-call(f32[256,2048]{1,0:T(8,128)} %get-tuple-element.42.gw3, f32[256,2048]{1,0:T(8,128)} %get-tuple-element.43.gw2, ...), custom_call_target="tpu_custom_call" | custom-call | tf_op jit(solution)/shard_map/emit/pallas_call | solution.py:727

commit v4 on v3

--- a/solution.py
+++ b/solution.py
@@ -112,7 +112,6 @@
         whole[e, :, span(core, width)] = functools.reduce(jnp.add, [chips[e, k] for k in range(DEVICES // 2)])
         share(e).start()
         share(e).wait()
-        return whole[e]
     return start, middle, take
 
 
@@ -127,15 +126,20 @@
         copy.wait()
 
 
-def backward_kernel(rows_total, dz, dz_pair, x2, x2_pair, x1, x1_pair, h_a, h_b, w3, w2, u2, u1, vec2, vec1,
+def backward_kernel(rows_total, dz, dz_pair, x2, x2_pair, x1, x1_pair, h_a, h_b, w3, w2, u2, u1, vec2_hbm, vec1_hbm,
                     gw3, gw2, gw1, sums2, sums1,
-                    d, pd, xt, hv, hturn, ht, dpre, wbuf, nbuf, acc3, acc2, acc1, near3, near2, near1, far3, far2, far1,
-                    mine, mate, chips, whole, load_sem, tile_sem, pair_send, pair_recv, hop_send, hop_recv, far_send, far_recv,
+                    vec2, vec1, d, pd, xt, hv, hturn, ht, dpre, wbuf, nbuf, acc3, acc2, acc1, near3, near2, near1, far3, far2, far1,
+                    mine, mate, chips, whole, vec_sem, load_sem, tile_sem, pair_send, pair_recv, hop_send, hop_recv, far_send, far_recv,
                     sum_send, sum_recv, h_send, h_recv, out_sem, w_sem, n_sem, free_sem):
     me = lax.axis_index("data")
     rows = d.shape[0]
     half = rows // 2
     greet()
+
+    def small(src, dst, k):
+        return pltpu.make_async_copy(src, dst, vec_sem.at[k])
+
+    vectors_in = [small(vec2_hbm, vec2, 0), small(vec1_hbm, vec1, 1)]
     send_sums, pass_sums, take_sums = exchange_halves(mine, mate, chips, whole, sum_send, sum_recv)
 
     def pair_copy(n, src=d):
@@ -278,9 +282,10 @@
     first = run(operand(x2, x2_pair))
     run([pltpu.make_async_copy(dz_pair.at[:, cols(k)], pd.at[:, cols(n)], pair_recv.at[n]) for k, n in enumerate(heads)])
     both_colours(lambda n, colour: dz_tile(n).start())
+    run(vectors_in)
     all_entered()
     run(passed)
-    finish_all(first)
+    finish_all(first + vectors_in)
     everything = ([(0, len(ORDER))],) * 2
     prod3.compute(([(1, 2)], [(2, 2)]), dz_arrived, True)
     back_product(w3, u2, vec2, 0)
@@ -294,8 +299,9 @@
     own_h = run([load(src, hv.at[span(v, half)], len(ORDER) + 1 + v) for v, src in views])
     pair_h = run([remote(src, hv.at[span(2 + v, half)], h_send.at[v], h_recv.at[v], PAIR) for v, src in views])
     prod3.relay()
-    sums2[...] = take_sums(0)
-    norm_grad(u2, vec2, sums2)
+    take_sums(0)
+    sums_out = run([small(whole.at[0], sums2, 2)])
+    norm_grad(u2, vec2, whole.at[0])
     finish_all(second)
     prod2.compute(everything, lambda n: pair_copy(n).wait(), True)
     pl.semaphore_signal(free_sem, inc=1, device_id=(me ^ PAIR,), device_id_type=MESH)
@@ -309,18 +315,20 @@
     pass_sums(1)
     prod3.finish()
     prod2.relay()
-    sums1[...] = take_sums(1)
+    take_sums(1)
+    sums_out += run([small(whole.at[1], sums1, 3)])
     pl.semaphore_wait(free_sem, 1)
-    norm_grad(u1, vec1, sums1)
+    norm_grad(u1, vec1, whole.at[1])
     prod1.compute(everything, lambda n: pair_copy(n).wait(), True)
     prod1.relay()
     prod2.finish()
     prod1.finish()
     for product in (prod3, prod2, prod1):
         product.drain()
-
-
-ANYWHERE, ON_CHIP = pl.BlockSpec(memory_space=pl.ANY), pl.BlockSpec(memory_space=pltpu.VMEM)
+    finish_all(sums_out)
+
+
+ANYWHERE = pl.BlockSpec(memory_space=pl.ANY)
 SCALARS = pl.BlockSpec(memory_space=pltpu.SMEM)
 
 
@@ -343,9 +351,9 @@
     return pl.pallas_call(
         functools.partial(backward_kernel, rows_total),
         out_shape=[jax.ShapeDtypeStruct((b, feats), F32) for b in blocks] + [sums, sums],
-        in_specs=[ANYWHERE] * (len(rest) - 1) + [ON_CHIP] * 2,
-        out_specs=[ANYWHERE] * WEIGHTS + [ON_CHIP] * 2,
-        scratch_shapes=[pltpu.VMEM((rows, feats), BF16), pltpu.VMEM((rows, feats), BF16),
+        in_specs=[ANYWHERE] * (len(rest) + 1),
+        out_specs=[ANYWHERE] * (WEIGHTS + 2),
+        scratch_shapes=[pltpu.VMEM((VEC_ROWS, feats), F32)] * 2 + [pltpu.VMEM((rows, feats), BF16), pltpu.VMEM((rows, feats), BF16),
                         pltpu.VMEM((2 * rows, groups * blk3), BF16), pltpu.VMEM((2 * rows, h_a.shape[1]), BF16),
                         pltpu.VMEM((h_a.shape[1], 2 * rows), BF16), pltpu.VMEM((groups * blk1, 2 * rows), BF16),
                         pltpu.VMEM((rows, feats), F32),
@@ -353,7 +361,7 @@
         + per_weight(groups) + per_weight(2) + per_weight(1)
         + [pltpu.VMEM(shape, F32) for shape in ((2,) + sums.shape, (2,) + half_sums, (2, DEVICES // 2) + half_sums,
                                                 (2,) + sums.shape)]
-        + [DMA((DEVICES,)), DMA((TILES,))]
+        + [DMA((len(ORDER),)), DMA((DEVICES,)), DMA((TILES,))]
         + [DMA((TILES,))] * 2 + [DMA((WEIGHTS, TILES))] * 4 + [DMA((2, DEVICES))] * 2 + [DMA((2,))] * 2
         + [DMA((WEIGHTS, TILES))] + [DMA((2,))] * 2 + [pltpu.SemaphoreType.REGULAR],
         compiler_params=params(cid),
@@ -362,8 +370,8 @@
 
 
 def forward_kernel(rows_total, lam, h_a, h_b, w1, w2, w3, gain1, shift1, gain2, shift2,
-                   loss, u1, u2, x1, x2, x1_pair, x2_pair, dz, dz_pair, vec1, vec2,
-                   hv, ubuf, vbuf, w2buf, w3buf, xbuf, zh, za, zb, corr, mine, slots, vec3, loss_mine, loss_slots,
+                   loss, u1, u2, x1, x2, x1_pair, x2_pair, dz, dz_pair, vec1_out, vec2_out,
+                   affine, vec1, vec2, vec_sem, hv, ubuf, vbuf, w2buf, w3buf, xbuf, zh, za, zb, corr, mine, slots, vec3, loss_mine, loss_slots,
                    load_sem, store_sem, pair_send, pair_recv, sum_send, sum_recv, za_send, za_recv, zb_send, zb_recv,
                    g_send, g_recv, loss_send, loss_recv, dz_sem, dz_send, dz_recv):
     me = lax.axis_index("data")
@@ -377,6 +385,8 @@
 
     w1_view = w3buf.at[pl.ds(0, w1.shape[0])]
     loads = run([load(h_a, hv.at[span(0, half)], 0), load(h_b, hv.at[span(1, half)], 1), load(w1, w1_view, 2)])
+    affine_in = run([pltpu.make_async_copy(src, affine.at[k], vec_sem.at[k])
+                     for k, src in enumerate((gain1, shift1, gain2, shift2))])
     all_entered()
     send_sums, take_sums = exchange(mine, slots, sum_send, sum_recv)
     send_loss, take_loss = exchange(loss_mine, loss_slots, loss_send, loss_recv)
@@ -421,10 +431,10 @@
             remote(xbuf.at[:, span(me ^ mask ^ PAIR, blk)], pair.at[:, pl.ds(j * blk, blk)],
                    pair_send.at[index, j], pair_recv.at[index, j], PAIR) for j, mask in enumerate(ORDER)])
 
-    for vec, gain, shift in ((vec1, gain1, shift1), (vec2, gain2, shift2)):
-        vec[pl.ds(GAIN, 1), :] = gain[...]
-        vec[pl.ds(SHIFT, 1), :] = shift[...]
-    finish_all(loads)
+    finish_all(loads + affine_in)
+    for k, vec in enumerate((vec1, vec2)):
+        vec[pl.ds(GAIN, 1), :] = affine[2 * k]
+        vec[pl.ds(SHIFT, 1), :] = affine[2 * k + 1]
     load_w2 = load(w2, w2buf, 0)
     load_w2.start()
     for v in TWO:
@@ -450,6 +460,9 @@
         if v:
             kept = keep_rows(x2, x2_pair, 1)
         layer(4 + v, v, xbuf, w3buf, ubuf)
+
+    small_out = run([pltpu.make_async_copy(vec, out, vec_sem.at[k])
+                     for k, (vec, out) in enumerate(((vec1, vec1_out), (vec2, vec2_out)))])
 
     def embed(v):
         take_vectors(4 + v, v, vec3)
@@ -642,7 +655,8 @@
 
     dz_sums(True)
     finish_all(kept)
-    loss[...] = take_loss(0)
+    loss_mine[0] = take_loss(0)
+    small_out += run([pltpu.make_async_copy(loss_mine.at[0], loss, vec_sem.at[2])])
     for v in TWO:
         slots[DG + v, me] = mine[DG + v]
     for v in TWO:
@@ -675,6 +689,7 @@
         copy.wait_send()
     for copy in started[-len(heads):]:
         copy.wait_recv()
+    finish_all(small_out)
     each_tile(lambda n, c: dz_copy(n).wait())
 
 
@@ -692,9 +707,10 @@
     return pl.pallas_call(
         functools.partial(forward_kernel, rows_total),
         out_shape=[jax.ShapeDtypeStruct(*out) for out in outs],
-        in_specs=[SCALARS] + [ANYWHERE] * 5 + [ON_CHIP] * len(vectors),
-        out_specs=[ON_CHIP] + [ANYWHERE] * (len(outs) - WEIGHTS) + [ON_CHIP] * 2,
-        scratch_shapes=[pltpu.VMEM(*item) for item in scratch]
+        in_specs=[SCALARS] + [ANYWHERE] * (5 + len(vectors)),
+        out_specs=[ANYWHERE] * len(outs),
+        scratch_shapes=[pltpu.VMEM((len(vectors), 1, feats), F32)] + [pltpu.VMEM(vec, F32)] * 2
+        + [DMA((len(vectors),))] + [pltpu.VMEM(*item) for item in scratch]
         + [DMA((WEIGHTS,))] * 2 + [DMA((2, len(ORDER)))] * 2 + [DMA((DEVICES + 2, DEVICES))] * 2 + [DMA((DEVICES,))] * 2
         + [DMA((DEVICES, 2))] * 2 + [DMA((DEVICES, 4))] * 2 + [DMA((1, DEVICES))] * 2 + [DMA((TILES,))] + [DMA((2,))] * 2,
         compiler_params=params(cid),
@@ -702,35 +718,46 @@
     )(lam, h_a, h_b, w1, w2, w3, *vectors)
 
 
-def emit_kernel(gw3, gw2, gw1, sums2, sums1, loss, loss_out, out3, out2, out1, gain1, shift1, gain2, shift2, buf, in_sem, out_sem):
+def emit_kernel(gw3, gw2, gw1, sums2, sums1, loss, loss_out, out3, out2, out1, gain1, shift1, gain2, shift2,
+                buf, sums, vecs, in_sem, out_sem, sum_sem, vec_sem):
     step = gw1.shape[0]
     pieces = [(src, dst, k) for src, dst in ((gw3, out3), (gw2, out2), (gw1, out1)) for k in range(src.shape[0] // step)]
     ins = run([pltpu.make_async_copy(src.at[span(k, step)], buf.at[i], in_sem.at[i])
                for i, (src, dst, k) in enumerate(pieces)])
+    sums_in = run([pltpu.make_async_copy(src, sums.at[i], sum_sem.at[i]) for i, src in enumerate((sums1, sums2))])
     outs = [pltpu.make_async_copy(buf.at[i], dst.at[span(k, step)], out_sem.at[i])
             for i, (src, dst, k) in enumerate(pieces)]
-    for sums, gain, shift in ((sums1, gain1, shift1), (sums2, gain2, shift2)):
-        both = sums[:2, :] + sums[2:, :]
-        shift[...] = both[:1]
-        gain[...] = both[1:]
     loss_out[0, 0] = loss[0, 0]
-    for before, after in zip(ins, outs):
+    half = len(ins) // 2
+    for before, after in zip(ins[:half], outs):
         before.wait()
         after.start()
-    finish_all(outs)
+    finish_all(sums_in)
+    for i in TWO:
+        both = sums[i, :2, :] + sums[i, 2:, :]
+        vecs[2 * i] = both[1:]
+        vecs[2 * i + 1] = both[:1]
+    vecs_out = run([pltpu.make_async_copy(vecs.at[i], dst, vec_sem.at[i])
+                    for i, dst in enumerate((gain1, shift1, gain2, shift2))])
+    for before, after in zip(ins[half:], outs[half:]):
+        before.wait()
+        after.start()
+    finish_all(outs + vecs_out)
 
 
 def emit(gw3, gw2, gw1, sums2, sums1, loss):
     weights = (gw3, gw2, gw1)
     step, feats = gw1.shape
     count = sum(g.shape[0] for g in weights) // step
+    vectors = [jax.ShapeDtypeStruct((1, feats), F32)] * 4
     return pl.pallas_call(
         emit_kernel,
-        out_shape=[jax.ShapeDtypeStruct((1, 1), F32)] + [jax.ShapeDtypeStruct(g.shape, F32) for g in weights]
-        + [jax.ShapeDtypeStruct((1, feats), F32)] * 4,
-        in_specs=[ANYWHERE] * WEIGHTS + [ON_CHIP] * 2 + [SCALARS],
-        out_specs=[SCALARS] + [ANYWHERE] * WEIGHTS + [ON_CHIP] * 4,
-        scratch_shapes=[pltpu.VMEM((count, step, feats), F32)] + [DMA((count,))] * 2,
+        out_shape=[jax.ShapeDtypeStruct((1, 1), F32)] + [jax.ShapeDtypeStruct(g.shape, F32) for g in weights] + vectors,
+        in_specs=[ANYWHERE] * (WEIGHTS + 2) + [SCALARS],
+        out_specs=[SCALARS] + [ANYWHERE] * (WEIGHTS + len(vectors)),
+        scratch_shapes=[pltpu.VMEM((count, step, feats), F32), pltpu.VMEM((2,) + sums1.shape, F32),
+                        pltpu.VMEM((len(vectors), 1, feats), F32)]
+        + [DMA((count,))] * 2 + [DMA((2,)), DMA((len(vectors),))],
         name="emit",
     )(*weights, sums2, sums1, loss)
 

time: 334 us -> 333 us (level)
  no operation moved by 1% of the time
where the time goes in v4:
time: 333 us; the launch traced here: 332 us
  Pallas kernels  331 us (99%)
    pallas_call x1, Pallas kernels, backward(): pl.pallas_call(functools.partial(backward_kernel, rows_total), out_shape=...  164 us
    pallas_call x1, Pallas kernels, forward(): pl.pallas_call(functools.partial(forward_kernel, rows_total), out_shape=[...  161 us

profile of v4, /device:TPU:0, one launch (start us, length us, event | category | flops | bytes accessed | tf_op | source)
XLA Modules:
  0.0 332.1 jit_solution(1984325990937458728)
XLA Ops:
  1.3 160.9 %forward.1 = (f32[8,128]{1,0:T(8,128)}, f32[1024,2048]{1,0:T(8,128)}, f32[1024,2048]{1,0:T(8,128)}, bf16[1024,2048]{1,0:T(8,128)(2,1)}, bf16[1024,2048]{1,0:T(8,...) custom-call(f32[1]{0:T(128)} %bitcast.10.lam, ...), custom_call_target="tpu_custom_call" | custom-call | tf_op jit(solution)/shard_map/forward/pallas_call | solution.py:707
  162.2 163.8 %backward.1 = (f32[256,2048]{1,0:T(8,128)}, f32[256,2048]{1,0:T(8,128)}, f32[64,2048]{1,0:T(8,128)}, f32[4,2048]{1,0:T(4,128)}, f32[4,2048]{1,0:T(4,128)}) custom-call(bf16[1024,2048]{1,0:T(8,128)(2,1)} %get-tuple-element.32.dz, bf16[1024,512]{1,0:T(8,128)(2,1)} %get-tuple-element.33.dz_pair, bf16[1024,2048]{1,0:T(8,128)(2,1)} %get-tuple-element.34.x2, ...), custom_call_target="tpu_custom_call" | custom-call | tf_op jit(solution)/shard_map/backward/pallas_call | solution.py:351
  326.0 5.9 %emit.1 = (f32[1,1]{1,0:T(1,128)}, f32[256,2048]{1,0:T(8,128)}, f32[256,2048]{1,0:T(8,128)}, f32[64,2048]{1,0:T(8,128)}, f32[1,2048]{1,0:T(1,128)}, /*index=5*/f...) custom-call(f32[256,2048]{1,0:T(8,128)} %get-tuple-element.42.gw3, f32[256,2048]{1,0:T(8,128)} %get-tuple-element.43.gw2, ...), custom_call_target="tpu_custom_call" | custom-call | tf_op jit(solution)/shard_map/emit/pallas_call | solution.py:753

commit v5 on v4

--- a/solution.py
+++ b/solution.py
@@ -16,6 +16,7 @@
 TWO = range(2)
 TILE = 256
 TILES = 8
+WIDE = 512
 WEIGHTS = 3
 GAIN, SHIFT, INV, MEAN, VEC_ROWS = 0, 1, 2, 4, 6
 VMEM_BYTES = 67043328
@@ -403,24 +404,29 @@
         vec[pl.ds(MEAN + v, 1), :] = mean
         vec[pl.ds(INV + v, 1), :] = lax.rsqrt(total[1:] - mean * mean + NORM_EPS)
 
-    def layer(e, v, left, weight, out):
+    def layer(e, v, left, weight, out, beside=None):
         part = span(v, half)
 
-        def body(n, c):
+        def body(n, carry):
+            c = span(n, WIDE)
             value = dot(left[part, :], weight[:, c])
             out[part, c] = value
             column_sums(mine, (e,), 0, c, value, value * value)
-        each_tile(body)
+            if beside:
+                beside(c)
+            return carry
+        lax.fori_loop(0, feats // WIDE, body, 0)
         send_sums(e)
 
     def normed_tile(values, v, c, vec):
         return (values[span(v, half), c] - row(vec, MEAN + v, c)) * row(vec, INV + v, c)
 
+    def activate_tile(v, values, vec, c):
+        pre = row(vec, GAIN, c) * normed_tile(values, v, c, vec) + row(vec, SHIFT, c)
+        xbuf[span(v, half), c] = jnp.maximum(pre, 0.0).astype(BF16)
+
     def activate(v, values, vec):
-        def body(n, c):
-            pre = row(vec, GAIN, c) * normed_tile(values, v, c, vec) + row(vec, SHIFT, c)
-            xbuf[span(v, half), c] = jnp.maximum(pre, 0.0).astype(BF16)
-        each_tile(body)
+        each_tile(lambda n, c: activate_tile(v, values, vec, c))
 
     def store(src, dst, k):
         return pltpu.make_async_copy(src, dst, store_sem.at[k])
@@ -442,15 +448,13 @@
     load_w3 = load(w3, w3buf, 2)
     store_u1 = store(ubuf, u1, 0)
     run([load_w3, store_u1])
-    kept = []
     for v in TWO:
         take_vectors(v, v, vec1)
-        activate(v, ubuf, vec1)
-        if v:
-            kept = keep_rows(x1, x1_pair, 0)
-        else:
-            load_w2.wait()
-        layer(2 + v, v, xbuf, w2buf, vbuf)
+    activate(0, ubuf, vec1)
+    load_w2.wait()
+    layer(2, 0, xbuf, w2buf, vbuf, functools.partial(activate_tile, 1, ubuf, vec1))
+    kept = keep_rows(x1, x1_pair, 0)
+    layer(3, 1, xbuf, w2buf, vbuf)
     store_u2 = store(vbuf, u2, 1)
     store_u2.start()
     finish_all([store_u1, load_w3] + kept)
@@ -719,7 +723,7 @@
 
 
 def emit_kernel(gw3, gw2, gw1, sums2, sums1, loss, loss_out, out3, out2, out1, gain1, shift1, gain2, shift2,
-                buf, sums, vecs, in_sem, out_sem, sum_sem, vec_sem):
+                buf, sums, vecs, loss_in, in_sem, out_sem, sum_sem, vec_sem, loss_sem):
     step = gw1.shape[0]
     pieces = [(src, dst, k) for src, dst in ((gw3, out3), (gw2, out2), (gw1, out1)) for k in range(src.shape[0] // step)]
     ins = run([pltpu.make_async_copy(src.at[span(k, step)], buf.at[i], in_sem.at[i])
@@ -727,7 +731,8 @@
     sums_in = run([pltpu.make_async_copy(src, sums.at[i], sum_sem.at[i]) for i, src in enumerate((sums1, sums2))])
     outs = [pltpu.make_async_copy(buf.at[i], dst.at[span(k, step)], out_sem.at[i])
             for i, (src, dst, k) in enumerate(pieces)]
-    loss_out[0, 0] = loss[0, 0]
+    loss_copy = pltpu.make_async_copy(loss, loss_in, loss_sem)
+    loss_copy.start()
     half = len(ins) // 2
     for before, after in zip(ins[:half], outs):
         before.wait()
@@ -742,6 +747,8 @@
     for before, after in zip(ins[half:], outs[half:]):
         before.wait()
         after.start()
+    loss_copy.wait()
+    loss_out[0, 0] = loss_in[0, 0]
     finish_all(outs + vecs_out)
 
 
@@ -753,11 +760,11 @@
     return pl.pallas_call(
         emit_kernel,
         out_shape=[jax.ShapeDtypeStruct((1, 1), F32)] + [jax.ShapeDtypeStruct(g.shape, F32) for g in weights] + vectors,
-        in_specs=[ANYWHERE] * (WEIGHTS + 2) + [SCALARS],
+        in_specs=[ANYWHERE] * (WEIGHTS + WEIGHTS),
         out_specs=[SCALARS] + [ANYWHERE] * (WEIGHTS + len(vectors)),
         scratch_shapes=[pltpu.VMEM((count, step, feats), F32), pltpu.VMEM((2,) + sums1.shape, F32),
-                        pltpu.VMEM((len(vectors), 1, feats), F32)]
-        + [DMA((count,))] * 2 + [DMA((2,)), DMA((len(vectors),))],
+                        pltpu.VMEM((len(vectors), 1, feats), F32), pltpu.SMEM(loss.shape, F32)]
+        + [DMA((count,))] * 2 + [DMA((2,)), DMA((len(vectors),)), DMA],
         name="emit",
     )(*weights, sums2, sums1, loss)
 

time: 333 us -> 330 us (level)
  no operation moved by 1% of the time
where the time goes in v5:
time: 330 us; the launch traced here: 329 us
  Pallas kernels  328 us (99%)
    pallas_call x1, Pallas kernels, backward(): pl.pallas_call(functools.partial(backward_kernel, rows_total), out_shape=...  164 us
    pallas_call x1, Pallas kernels, forward(): pl.pallas_call(functools.partial(forward_kernel, rows_total), out_shape=[...  159 us

profile of v5, /device:TPU:0, one launch (start us, length us, event | category | flops | bytes accessed | tf_op | source)
XLA Modules:
  0.0 329.2 jit_solution(10163648757351021049)
XLA Ops:
  1.3 158.8 %forward.1 = (f32[8,128]{1,0:T(8,128)}, f32[1024,2048]{1,0:T(8,128)}, f32[1024,2048]{1,0:T(8,128)}, bf16[1024,2048]{1,0:T(8,128)(2,1)}, bf16[1024,2048]{1,0:T(8,...) custom-call(f32[1]{0:T(128)} %bitcast.10.lam, ...), custom_call_target="tpu_custom_call" | custom-call | tf_op jit(solution)/shard_map/forward/pallas_call | solution.py:711
  160.0 163.8 %backward.1 = (f32[256,2048]{1,0:T(8,128)}, f32[256,2048]{1,0:T(8,128)}, f32[64,2048]{1,0:T(8,128)}, f32[4,2048]{1,0:T(4,128)}, f32[4,2048]{1,0:T(4,128)}) custom-call(bf16[1024,2048]{1,0:T(8,128)(2,1)} %get-tuple-element.32.dz, bf16[1024,512]{1,0:T(8,128)(2,1)} %get-tuple-element.33.dz_pair, bf16[1024,2048]{1,0:T(8,128)(2,1)} %get-tuple-element.34.x2, ...), custom_call_target="tpu_custom_call" | custom-call | tf_op jit(solution)/shard_map/backward/pallas_call | solution.py:352
  323.8 5.2 %emit.1 = (f32[1,1]{1,0:T(1,128)}, f32[256,2048]{1,0:T(8,128)}, f32[256,2048]{1,0:T(8,128)}, f32[64,2048]{1,0:T(8,128)}, f32[1,2048]{1,0:T(1,128)}, /*index=5*/f...) custom-call(f32[256,2048]{1,0:T(8,128)} %get-tuple-element.42.gw3, f32[256,2048]{1,0:T(8,128)} %get-tuple-element.43.gw2, ...), custom_call_target="tpu_custom_call" | custom-call | tf_op jit(solution)/shard_map/emit/pallas_call | solution.py:760

commit v6 on v5

--- a/solution.py
+++ b/solution.py
@@ -388,7 +388,6 @@
     loads = run([load(h_a, hv.at[span(0, half)], 0), load(h_b, hv.at[span(1, half)], 1), load(w1, w1_view, 2)])
     affine_in = run([pltpu.make_async_copy(src, affine.at[k], vec_sem.at[k])
                      for k, src in enumerate((gain1, shift1, gain2, shift2))])
-    all_entered()
     send_sums, take_sums = exchange(mine, slots, sum_send, sum_recv)
     send_loss, take_loss = exchange(loss_mine, loss_slots, loss_send, loss_recv)
 
@@ -416,7 +415,6 @@
                 beside(c)
             return carry
         lax.fori_loop(0, feats // WIDE, body, 0)
-        send_sums(e)
 
     def normed_tile(values, v, c, vec):
         return (values[span(v, half), c] - row(vec, MEAN + v, c)) * row(vec, INV + v, c)
@@ -445,6 +443,9 @@
     load_w2.start()
     for v in TWO:
         layer(v, v, hv, w1_view, ubuf)
+    all_entered()
+    for v in TWO:
+        send_sums(v)
     load_w3 = load(w3, w3buf, 2)
     store_u1 = store(ubuf, u1, 0)
     run([load_w3, store_u1])
@@ -453,8 +454,10 @@
     activate(0, ubuf, vec1)
     load_w2.wait()
     layer(2, 0, xbuf, w2buf, vbuf, functools.partial(activate_tile, 1, ubuf, vec1))
+    send_sums(2)
     kept = keep_rows(x1, x1_pair, 0)
     layer(3, 1, xbuf, w2buf, vbuf)
+    send_sums(3)
     store_u2 = store(vbuf, u2, 1)
     store_u2.start()
     finish_all([store_u1, load_w3] + kept)
@@ -464,6 +467,7 @@
         if v:
             kept = keep_rows(x2, x2_pair, 1)
         layer(4 + v, v, xbuf, w3buf, ubuf)
+        send_sums(4 + v)
 
     small_out = run([pltpu.make_async_copy(vec, out, vec_sem.at[k])
                      for k, (vec, out) in enumerate(((vec1, vec1_out), (vec2, vec2_out)))])

time: 330 us -> 331 us (level)
  no operation moved by 1% of the time
where the time goes in v6:
time: 331 us
  Pallas kernels  329 us (99%)
    pallas_call x1, Pallas kernels, backward(): pl.pallas_call(functools.partial(backward_kernel, rows_total), out_shape=...  164 us
    pallas_call x1, Pallas kernels, forward(): pl.pallas_call(functools.partial(forward_kernel, rows_total), out_shape=[...  160 us

profile of v6, /device:TPU:0, one launch (start us, length us, event | category | flops | bytes accessed | tf_op | source)
XLA Modules:
  0.0 330.6 jit_solution(2801896854824672644)
XLA Ops:
  1.3 160.1 %forward.1 = (f32[8,128]{1,0:T(8,128)}, f32[1024,2048]{1,0:T(8,128)}, f32[1024,2048]{1,0:T(8,128)}, bf16[1024,2048]{1,0:T(8,128)(2,1)}, bf16[1024,2048]{1,0:T(8,...) custom-call(f32[1]{0:T(128)} %bitcast.10.lam, ...), custom_call_target="tpu_custom_call" | custom-call | tf_op jit(solution)/shard_map/forward/pallas_call | solution.py:715
  161.4 163.8 %backward.1 = (f32[256,2048]{1,0:T(8,128)}, f32[256,2048]{1,0:T(8,128)}, f32[64,2048]{1,0:T(8,128)}, f32[4,2048]{1,0:T(4,128)}, f32[4,2048]{1,0:T(4,128)}) custom-call(bf16[1024,2048]{1,0:T(8,128)(2,1)} %get-tuple-element.32.dz, bf16[1024,512]{1,0:T(8,128)(2,1)} %get-tuple-element.33.dz_pair, bf16[1024,2048]{1,0:T(8,128)(2,1)} %get-tuple-element.34.x2, ...), custom_call_target="tpu_custom_call" | custom-call | tf_op jit(solution)/shard_map/backward/pallas_call | solution.py:352
  325.2 5.2 %emit.1 = (f32[1,1]{1,0:T(1,128)}, f32[256,2048]{1,0:T(8,128)}, f32[256,2048]{1,0:T(8,128)}, f32[64,2048]{1,0:T(8,128)}, f32[1,2048]{1,0:T(1,128)}, /*index=5*/f...) custom-call(f32[256,2048]{1,0:T(8,128)} %get-tuple-element.42.gw3, f32[256,2048]{1,0:T(8,128)} %get-tuple-element.43.gw2, ...), custom_call_target="tpu_custom_call" | custom-call | tf_op jit(solution)/shard_map/emit/pallas_call | solution.py:764

commit v7 on v5

--- a/solution.py
+++ b/solution.py
@@ -404,7 +404,7 @@
         vec[pl.ds(MEAN + v, 1), :] = mean
         vec[pl.ds(INV + v, 1), :] = lax.rsqrt(total[1:] - mean * mean + NORM_EPS)
 
-    def layer(e, v, left, weight, out, beside=None):
+    def layer(e, v, left, weight, out, beside=None, tiles=None):
         part = span(v, half)
 
         def body(n, carry):
@@ -415,8 +415,9 @@
             if beside:
                 beside(c)
             return carry
-        lax.fori_loop(0, feats // WIDE, body, 0)
-        send_sums(e)
+        lax.fori_loop(*(tiles or (0, feats // WIDE)), body, 0)
+        if not tiles or tiles[1] == feats // WIDE:
+            send_sums(e)
 
     def normed_tile(values, v, c, vec):
         return (values[span(v, half), c] - row(vec, MEAN + v, c)) * row(vec, INV + v, c)
@@ -458,22 +459,24 @@
     store_u2 = store(vbuf, u2, 1)
     store_u2.start()
     finish_all([store_u1, load_w3] + kept)
-    for v in TWO:
-        take_vectors(2 + v, v, vec2)
-        activate(v, vbuf, vec2)
-        if v:
-            kept = keep_rows(x2, x2_pair, 1)
-        layer(4 + v, v, xbuf, w3buf, ubuf)
-
+    take_vectors(2, 0, vec2)
+    activate(0, vbuf, vec2)
+    count = feats // WIDE
+    middle = count // 2
+    layer(4, 0, xbuf, w3buf, ubuf, None, (0, middle))
+    take_vectors(3, 1, vec2)
+
+    def activate_two(c):
+        for k in TWO:
+            activate_tile(1, vbuf, vec2, pl.ds(pl.multiple_of((c.start - middle * WIDE) * 2 + k * WIDE, WIDE), WIDE))
+    layer(4, 0, xbuf, w3buf, ubuf, activate_two, (middle, count))
+    kept = keep_rows(x2, x2_pair, 1)
+    layer(5, 1, xbuf, w3buf, ubuf, None, (0, count - 1))
     small_out = run([pltpu.make_async_copy(vec, out, vec_sem.at[k])
                      for k, (vec, out) in enumerate(((vec1, vec1_out), (vec2, vec2_out)))])
 
-    def embed(v):
-        take_vectors(4 + v, v, vec3)
-
-        def body(n, c):
-            zh[span(v, half), c] = normed_tile(ubuf, v, c, vec3).astype(BF16)
-        each_tile(body)
+    def embed_tile(v, c):
+        zh[span(v, half), c] = normed_tile(ubuf, v, c, vec3).astype(BF16)
 
     def row_index(mask):
         dev = me ^ mask
@@ -520,10 +523,12 @@
     def accumulate(origin):
         corr[...] = corr[...] + dot(za[me ^ origin], zb[me ^ origin], TURN_LEFT)
 
-    embed(0)
+    take_vectors(4, 0, vec3)
+    layer(5, 1, xbuf, w3buf, ubuf, lambda c: [embed_tile(0, span(n, WIDE)) for n in range(count)], (count - 1, count))
     for mask in (YN, XN, YP, XP, PAIR):
         go(za_direct(mask))
-    embed(1)
+    take_vectors(5, 1, vec3)
+    each_tile(lambda n, c: embed_tile(1, c))
     for k in TWO:
         for mask in (XN, YN, PAIR):
             go(zb_direct(mask, k))

time: 330 us -> 331 us (level)
  no operation moved by 1% of the time
where the time goes in v7:
time: 331 us; the launch traced here: 330 us
  Pallas kernels  328 us (99%)
    pallas_call x1, Pallas kernels, backward(): pl.pallas_call(functools.partial(backward_kernel, rows_total), out_shape=...  164 us
    pallas_call x1, Pallas kernels, forward(): pl.pallas_call(functools.partial(forward_kernel, rows_total), out_shape=[...  159 us

profile of v7, /device:TPU:0, one launch (start us, length us, event | category | flops | bytes accessed | tf_op | source)
XLA Modules:
  0.0 329.9 jit_solution(11295842795082632398)
XLA Ops:
  1.3 159.4 %forward.1 = (f32[8,128]{1,0:T(8,128)}, f32[1024,2048]{1,0:T(8,128)}, f32[1024,2048]{1,0:T(8,128)}, bf16[1024,2048]{1,0:T(8,128)(2,1)}, bf16[1024,2048]{1,0:T(8,...) custom-call(f32[1]{0:T(128)} %bitcast.10.lam, ...), custom_call_target="tpu_custom_call" | custom-call | tf_op jit(solution)/shard_map/forward/pallas_call | solution.py:716
  160.7 163.7 %backward.1 = (f32[256,2048]{1,0:T(8,128)}, f32[256,2048]{1,0:T(8,128)}, f32[64,2048]{1,0:T(8,128)}, f32[4,2048]{1,0:T(4,128)}, f32[4,2048]{1,0:T(4,128)}) custom-call(bf16[1024,2048]{1,0:T(8,128)(2,1)} %get-tuple-element.32.dz, bf16[1024,512]{1,0:T(8,128)(2,1)} %get-tuple-element.33.dz_pair, bf16[1024,2048]{1,0:T(8,128)(2,1)} %get-tuple-element.34.x2, ...), custom_call_target="tpu_custom_call" | custom-call | tf_op jit(solution)/shard_map/backward/pallas_call | solution.py:352
  324.5 5.2 %emit.1 = (f32[1,1]{1,0:T(1,128)}, f32[256,2048]{1,0:T(8,128)}, f32[256,2048]{1,0:T(8,128)}, f32[64,2048]{1,0:T(8,128)}, f32[1,2048]{1,0:T(1,128)}, /*index=5*/f...) custom-call(f32[256,2048]{1,0:T(8,128)} %get-tuple-element.42.gw3, f32[256,2048]{1,0:T(8,128)} %get-tuple-element.43.gw2, ...), custom_call_target="tpu_custom_call" | custom-call | tf_op jit(solution)/shard_map/emit/pallas_call | solution.py:765
